TPU v7x, 512 devices: a whole 4x4x16 slice. The times are simulated.
512 devices in a mesh: dp: 64 (over z, y_lo, core), tensor: 8 (over x, y_hi).
Axes of the slice: x: 4, y: 4 (y_hi: 2, y_lo: 2; y = y_hi * 2 + y_lo), z: 16, core: 2. Of those that a mesh axis runs over, the one named last changes fastest.
Arguments:
- activations: bfloat16 [131072, 1024], P(('dp', 'tensor')), may hold values from -24 to 24
- gradients: bfloat16 [131072, 5472], P('dp', 'tensor'), may hold values from -6 to 6
- act_history: float32 [8, 16, 1024], P('tensor'), may hold values from 0.1 to 4
- grad_history: float32 [16, 5472], P(None, 'tensor'), may hold values from 0.1 to 4
- owner_rank: int32 [1024], replicated, may hold values from 0 to 7
- history_slot: int32 [6496], replicated, may hold values from 0 to 15
Outputs:
- weight_grad: float32 [1024, 5472], P('dp', 'tensor')
- act_history_out: float32 [8, 16, 1024], P('tensor')
- grad_history_out: float32 [16, 5472], P(None, 'tensor')
All inputs are finite; a program needn't handle non-finite values.
Results may differ from a plain program's by a relative error of at most 0.0042.
Values may be sent and summed in bfloat16 or wider, within the bound.
A program may use at most 64 MiB of HBM per device.

v0:
```python
import math

import jax
import jax.numpy as jnp
from jax import lax
from jax.sharding import PartitionSpec as P

QUANT_LIMIT = 448.0
SCALE_FLOOR = 0.25


def sent_to_all(value, axis):
    copies = jnp.broadcast_to(value, (lax.axis_size(axis), *value.shape))
    return lax.all_to_all(copies, axis, split_axis=0, concat_axis=0, tiled=True)


def of_everyone(value, axis):
    everything = sent_to_all(value, axis)
    return jnp.sum(everything, axis=0)


def cut_along(value, dim, length):
    lengths = value.shape
    parts = value.reshape(*lengths[:dim], length, lengths[dim] // length, *lengths[dim + 1 :])
    return jnp.moveaxis(parts, dim, 0)


def summed_on_arrival(value, axis, dim):
    length = lax.axis_size(axis)
    parts = lax.all_to_all(cut_along(value, dim, length), axis, 0, 0, tiled=True)
    return jnp.sum(parts.astype(jnp.float32), axis=0)


def taken_together(value, axis):
    everything = sent_to_all(value, axis)
    return jnp.max(everything, axis=0)


def in_one(arrays, axis):
    flat, at, done = (jnp.concatenate([a.reshape(-1) for a in arrays]), 0, [])
    subtotal = taken_together(flat, axis)
    for a in arrays:
        done.append(subtotal[at : at + a.size].reshape(a.shape))
        at += a.size
    return tuple(done)


def quantize(values, scale):
    scaled = values.astype(jnp.float32) * scale
    return jnp.clip(scaled, -QUANT_LIMIT, QUANT_LIMIT).astype(jnp.bfloat16)


def place_peaks(history, peaks, slots):
    rows = lax.broadcasted_iota(jnp.int32, history.shape, 0)
    return jnp.where(rows == slots[None, :], peaks[None, :], history)


def body(activations, gradients, act_history, grad_history, owner_rank, history_slot):
    model_width = act_history.shape[2]
    column_total = gradients.shape[1]
    my_rank = lax.axis_index("tensor")
    held = jnp.where(owner_rank[None, :] == my_rank, act_history[0], jnp.float32(0.0))
    current_history = of_everyone(held, "tensor")
    act_scale = QUANT_LIMIT / jnp.maximum(jnp.max(current_history, axis=0), SCALE_FLOOR)
    grad_scale = QUANT_LIMIT / jnp.maximum(jnp.max(grad_history, axis=0), SCALE_FLOOR)
    grad_quant = quantize(gradients, grad_scale)
    row_count = model_width // lax.axis_size("dp")
    grad_factor = 1.0 / math.sqrt(gradients.shape[0] * lax.axis_size("dp"))
    own_grad_peak = jnp.max(jnp.abs(gradients), axis=0).astype(jnp.float32)
    contract_rows = (((0,), (0,)), ((), ()))
    gathered_peak = jnp.zeros((model_width,), jnp.float32)
    act_piece = lax.all_gather(activations, "tensor", axis=0, tiled=True)
    running_peak = gathered_peak
    quantized = quantize(act_piece, act_scale)
    peak_next = jnp.maximum(running_peak, jnp.max(jnp.abs(act_piece), axis=0).astype(jnp.float32))
    partial_sum = lax.dot_general(
        quantized, grad_quant, contract_rows, preferred_element_type=jnp.float32
    )
    partial_sum, gathered_peak = (partial_sum, peak_next)
    summed = summed_on_arrival(partial_sum.astype(jnp.bfloat16), "dp", 0)
    act_peak, grad_peak = in_one((gathered_peak, own_grad_peak), "dp")
    row_base = lax.axis_index("dp") * row_count
    row_scale = lax.dynamic_slice_in_dim(act_scale, row_base, row_count, 0)
    weight_grad = summed / (row_scale[:, None] * grad_scale[None, :]) * grad_factor
    act_slots = history_slot[:model_width]
    grad_slots = lax.dynamic_slice_in_dim(
        history_slot, model_width + my_rank * column_total, column_total, 0
    )
    updated = place_peaks(current_history, act_peak, act_slots)
    act_history_out = updated[None]
    grad_history_out = place_peaks(grad_history, grad_peak, grad_slots)
    return (weight_grad, act_history_out, grad_history_out)


def solution(mesh):
    placed = (
        P(("dp", "tensor"), None),
        P("dp", "tensor"),
        P("tensor", None, None),
        P(None, "tensor"),
        P(),
        P(),
    )
    return jax.shard_map(
        body,
        mesh=mesh,
        in_specs=placed,
        out_specs=(P("dp", "tensor"), P("tensor", None, None), P(None, "tensor")),
        check_vma=False,
    )
```

profile of v0, /device:TPU:8, one launch (start us, length us, event | category | flops | bytes accessed | tf_op | source)
XLA Modules:
  0.0 252.6 jit_solution(7629873349470279669)
XLA Ops:
  7.2 0.0 all-gather.2.cloned.1.call-start
  7.2 0.7 all-gather.2.cloned.1.call-update
  7.9 0.7 broadcast_compare_fusion
  8.6 0.8 bitcast_select_fusion.1
  9.4 0.8 broadcast_in_dim.49
  10.3 6.0 %all-to-all-start = ((f32[8,16,1024]{2,1,0:T(8,128)}), f32[8,16,1024]{2,1,0:T(8,128)S(1)}, u32[]{:S(2)}, u32[]{:S(2)}) async-start(f32[8,16,1024]{2,1,0:T(8,128)} %broadcast_in_dim.49), calls=%async_computation | async-start | bytes 1048576 | tf_op jit(solution)/shard_map/all_to_all | solution.py:14
  16.3 0.0 copy-start
  16.3 2.6 %abs_reduce_fusion.1 = bf16[684]{0:T(1024)(128)(2,1)S(1)} fusion(bf16[2048,684]{0,1:T(8,128)(2,1)} %param.7), kind=kLoop, calls=%fused_computation.8 | loop fusion | flops 2800980 | bytes 2803032 | tf_op jit(solution)/shard_map/reduce_max | solution.py:69
  18.9 82.8 %all-gather.2.cloned.1.call-done = bf16[2048,1024]{1,0:T(8,128)(2,1)} async-done(((bf16[256,1024]{1,0:T(8,128)(2,1)}), bf16[2048,1024]{1,0:T(8,128)(2,1)}) %all-gather.2.cloned.1.call-update) | async-done | bytes 4194320 | tf_op jit(solution)/shard_map/all_gather | solution.py:72
  101.7 2.6 %abs_reduce_fusion = bf16[1024]{0:T(1024)(128)(2,1)S(1)} fusion(bf16[2048,1024]{1,0:T(8,128)(2,1)} %all-gather.2.cloned.1.call-done), kind=kLoop, calls=%fused_computation.3 | loop fusion | flops 4193280 | bytes 4196352 | tf_op jit(solution)/shard_map/reduce_max | solution.py:75
  104.4 1.0 broadcast_in_dim.51
  105.4 14.4 %all-to-all-start.2 = ((f32[64,1,1708]{2,1,0:T(1,128)}), f32[64,1,1708]{2,1,0:T(1,128)}, u32[]{:S(2)}, u32[]{:S(2)}) async-start(f32[64,1,1708]{2,1,0:T(1,128)} %broadcast_in_dim.51), calls=%async_computation.2 | async-start | bytes 917504 | tf_op jit(solution)/shard_map/all_to_all | solution.py:14
  119.8 0.1 dynamic_slice.7
  119.9 30.5 %all-to-all-done.2 = f32[64,1,1708]{2,1,0:T(1,128)} async-done(((f32[64,1,1708]{2,1,0:T(1,128)}), f32[64,1,1708]{2,1,0:T(1,128)}, u32[]{:S(2)}, u32[]{:S(2)}) %all-to-all-start.2) | async-done | bytes 437280 | tf_op jit(solution)/shard_map/all_to_all | solution.py:14
  150.4 1.3 reduce_max.49
  151.8 0.6 fusion.8
  152.4 6.5 %fusion.7 = bf16[1024,684]{0,1:T(8,128)(2,1)} fusion(bf16[2048,684]{0,1:T(8,128)(2,1)S(1)} %copy-done, f32[684]{0:T(1024)S(1)} %maximum_divide_fusion, bf16[2048,1024]{1,0:T(8,128)(2,1)} %all-gather.2.cloned.1.call-done, f32[1024]{0:T(1024)S(1)} %maximum_divide_fusion.1), kind=kOutput, calls=%fused_computation.12 | convolution fusion | flops 2883596288 | bytes 8403632 | tf_op jit(solution)/shard_map/dot_general | solution.py:76
  158.9 2.6 %copy.11 = bf16[1024,684]{1,0:T(8,128)(2,1)} copy(bf16[1024,684]{0,1:T(8,128)(2,1)} %fusion.7) | data formatting | bytes 2801664 | tf_op jit(solution)/shard_map/convert_element_type | solution.py:80
  161.5 4.7 %all-to-all-start.1 = ((bf16[64,16,684]{2,1,0:T(8,128)(2,1)}), bf16[64,16,684]{2,1,0:T(8,128)(2,1)S(1)}, u32[]{:S(2)}, u32[]{:S(2)}) async-start(bf16[64,16,684]{2,1,0:T(8,128)(2,1)} %bitcast.1), calls=%async_computation.1 | async-start | bytes 3145728 | tf_op jit(solution)/shard_map/all_to_all | solution.py:30
  166.2 0.1 dynamic_slice.6
  166.3 0.6 bitcast_select_fusion
  166.9 77.9 %all-to-all-done.1 = bf16[64,16,684]{2,1,0:T(8,128)(2,1)S(1)} async-done(((bf16[64,16,684]{2,1,0:T(8,128)(2,1)}), bf16[64,16,684]{2,1,0:T(8,128)(2,1)S(1)}, u32[]{:S(2)}, u32[]{:S(2)}) %all-to-all-start.1) | async-done | bytes 1400864 | tf_op jit(solution)/shard_map/all_to_all | solution.py:30
  244.8 0.3 convert_reduce_fusion
  245.1 0.7 divide_multiply_fusion
  (17 shorter events, 0.1 us)
Async XLA Ops:
  7.2 94.5 %all-gather.2.cloned.1.call-start = ((), (), s32[]{:S(2)}) async-start(), calls=%async_computation.3 | async-start | bytes 4718592 | tf_op jit(solution)/shard_map/all_gather | solution.py:72
  10.3 94.1 %all-to-all-start = ((f32[8,16,1024]{2,1,0:T(8,128)}), f32[8,16,1024]{2,1,0:T(8,128)S(1)}, u32[]{:S(2)}, u32[]{:S(2)}) async-start(f32[8,16,1024]{2,1,0:T(8,128)} %broadcast_in_dim.49), calls=%async_computation | async-start | bytes 1048576 | tf_op jit(solution)/shard_map/all_to_all | solution.py:14
  16.3 103.4 %copy-start.2 = (s32[6496]{0:T(1024)S(1)}, s32[6496]{0:T(1024)}, u32[]{:S(2)}) copy-start(s32[6496]{0:T(1024)} %param.11) | copy-start | bytes 77956
  16.3 135.4 %copy-start.1 = (f32[16,684]{1,0:T(8,128)S(1)}, f32[16,684]{1,0:T(8,128)}, u32[]{:S(2)}) copy-start(f32[16,684]{1,0:T(8,128)} %param.9) | copy-start | bytes 131332
  16.3 136.1 %copy-start = (bf16[2048,684]{0,1:T(8,128)(2,1)S(1)}, bf16[2048,684]{0,1:T(8,128)(2,1)}, u32[]{:S(2)}) copy-start(bf16[2048,684]{0,1:T(8,128)(2,1)} %param.7) | copy-start | bytes 8404996
  105.4 45.1 %all-to-all-start.2 = ((f32[64,1,1708]{2,1,0:T(1,128)}), f32[64,1,1708]{2,1,0:T(1,128)}, u32[]{:S(2)}, u32[]{:S(2)}) async-start(f32[64,1,1708]{2,1,0:T(1,128)} %broadcast_in_dim.51), calls=%async_computation.2 | async-start | bytes 917504 | tf_op jit(solution)/shard_map/all_to_all | solution.py:14
  158.9 7.4 %slice-start = ((s32[6496]{0:T(1024)}), s32[1024]{0:T(1024)S(1)}, s32[]{:S(2)}) async-start(s32[6496]{0:T(1024)} %param.11), calls=%async_computation.4 | async-start | bytes 8192 | tf_op jit(solution)/shard_map/slice | solution.py:85
  161.5 83.3 %all-to-all-start.1 = ((bf16[64,16,684]{2,1,0:T(8,128)(2,1)}), bf16[64,16,684]{2,1,0:T(8,128)(2,1)S(1)}, u32[]{:S(2)}, u32[]{:S(2)}) async-start(bf16[64,16,684]{2,1,0:T(8,128)(2,1)} %bitcast.1), calls=%async_computation.1 | async-start | bytes 3145728 | tf_op jit(solution)/shard_map/all_to_all | solution.py:30
Sparse Core Ops, SparseCore 0:
  11.2 90.4 all-gather.1
where the time goes:
time: 253 us
  waiting for transfers between devices  192 us (76%)
  starting transfers between devices  25.1 us (10%)
  between operations  14.1 us (6%)
  other arithmetic  10.3 us (4%)
  matrix products  6.51 us (3%)
  local copies, waits for them, and re-layouts  4.63 us (2%)
    all_gather x1, waiting for transfers between devices, body(): act_piece = lax.all_gather(activations, 'tensor', axis=0, tiled=True)  82.8 us
    all_to_all x1, waiting for transfers between devices, summed_on_arrival(): lax.all_to_all(cut_along(value, dim, length), axis, 0, 0, tiled=True)  77.9 us
    all_to_all x2, waiting for transfers between devices, sent_to_all(): return lax.all_to_all(copies, axis, split_axis=0, concat_axis=0, tiled=True)  30.5 us
    all_to_all x2, starting transfers between devices, sent_to_all(): return lax.all_to_all(copies, axis, split_axis=0, concat_axis=0, tiled=True)  20.4 us
    dot_general x1, matrix products, body(): lax.dot_general(quantized, grad_quant, contract_rows, preferred_element_t...  6.51 us
  transfers between devices with their start and end apart: 4, of which 3 were waited for; matrix products, arithmetic and copies ran while one was open for 3% of the time, Pallas kernels for 0%

commit v1 on v0

v1 whole, which is shorter than its diff:
```python
import functools
import math

import jax
import jax.numpy as jnp
from jax import lax
from jax.experimental import pallas as pl
from jax.experimental.pallas import tpu as pltpu
from jax.sharding import PartitionSpec as P

QUANT_LIMIT = 448.0
SCALE_FLOOR = 0.25
LANES = 128
MESH = pl.DeviceIdType.MESH


def kernel(
    nz, nx, acts, grads, ahist, ghist, owner,
    sum_out, hist_out, peak_out, gpeak_out, ascale_out, gscale_out,
    g, acol, graw, gq, q, scales, mh, msg, hr, hb, ch, pv, pcore, pylo, pz1, pz2,
    part, s1, r1, s2, r2, keep2, s3, rb,
    ld_g, ld_a, ld_r,
    sy, ry, sxo, rxo, sxp, rxp, sf, rf,
    sm, rm, sh1, rh1, sh3, rh3, sh4, rh4,
    sp2, rp2, sp3, rp3, sp4, rp4, sp5, rp5,
    sr1, rr1, sr2, rr2, sr3, rr3,
):
    nc = nz // 2
    nt = 2 * nx
    rows = acts.shape[0]
    width = grads.shape[1]
    pb = 4
    t = lax.axis_index("tensor")
    dpi = lax.axis_index("dp")
    x, yh = t // 2, t % 2
    z, yl, c = dpi // 4, (dpi // 2) % 2, dpi % 2
    q_slot = 2 * x + (1 - yh)
    xr, xl = (x + 1) % nx, (x + nx - 1) % nx

    def tensor_dev(tt):
        return {"dp": dpi, "tensor": tt}

    def dp_dev(zz, yy, cc):
        return {"dp": zz * 4 + yy * 2 + cc, "tensor": t}

    def rcopy(src, dst, ss, rs, device):
        return pltpu.make_async_remote_copy(
            src_ref=src, dst_ref=dst, send_sem=ss, recv_sem=rs,
            device_id=device, device_id_type=MESH,
        )

    def chunk(s):
        half = (s + 1) // 2
        return (z // 2 + nc // 2 + (1 - 2 * (s % 2)) * half + 2 * nc) % nc

    partner_y = tensor_dev(q_slot)
    right = tensor_dev(2 * xr + yh)
    left = tensor_dev(2 * xl + yh)
    other_core = dp_dev(z, yl, 1 - c)
    other_yl = dp_dev(z, 1 - yl, c)

    def load_g(s):
        col = pl.multiple_of(chunk(s) * LANES, LANES)
        return pltpu.make_async_copy(acts.at[:, pl.ds(col, LANES)], g.at[s, t], ld_g.at[s])

    for s in range(nc):
        load_g(s).start()
    load_a = pltpu.make_async_copy(acts, acol, ld_a)
    load_a.start()
    load_r = pltpu.make_async_copy(grads, graw, ld_r)
    load_r.start()

    bar = pltpu.get_barrier_semaphore()
    for i in range(1, nt):
        pl.semaphore_signal(bar, inc=1, device_id=tensor_dev((t + i) % nt), device_id_type=MESH)
    pl.semaphore_signal(bar, inc=1, device_id=other_core, device_id_type=MESH)
    pl.semaphore_signal(bar, inc=1, device_id=other_yl, device_id_type=MESH)
    for i in range(1, nz):
        pl.semaphore_signal(bar, inc=1, device_id=dp_dev((z + i) % nz, yl, c), device_id_type=MESH)

    held = jnp.where(owner[...] == t, ahist[0], jnp.float32(0.0))
    mh[...] = held
    msg[t, :, : nc * LANES] = jnp.max(held, axis=0, keepdims=True)
    hcol = pl.multiple_of((z % nc) * LANES, LANES)
    hrow = pl.multiple_of(c * 8, 8)
    hr[t] = mh[pl.ds(hrow, 8), pl.ds(hcol, LANES)]
    gscale = QUANT_LIMIT / jnp.maximum(jnp.max(ghist[...], axis=0, keepdims=True), SCALE_FLOOR)
    gscale_out[...] = gscale

    pl.semaphore_wait(bar, nt - 1 + 2 + nz - 1)

    def y_copy(s):
        return rcopy(g.at[s, t], g.at[s, t], sy.at[s], ry.at[s], partner_y)

    def y_arrival(s):
        return rcopy(g.at[s, q_slot], g.at[s, q_slot], sy.at[s], ry.at[s], partner_y)

    def xo_copy(s, d):
        return rcopy(g.at[s, t], g.at[s, t], sxo.at[s, d], rxo.at[s, d], right if d == 0 else left)

    def xp_copy(s, d):
        return rcopy(
            g.at[s, q_slot], g.at[s, q_slot], sxp.at[s, d], rxp.at[s, d], right if d == 0 else left
        )

    lo, lp = 2 * xl + yh, 2 * xl + 1 - yh
    ro, rp = 2 * xr + yh, 2 * xr + 1 - yh

    def xo_arrival(s, d):
        slot = lo if d == 0 else ro
        return rcopy(g.at[s, slot], g.at[s, slot], sxo.at[s, d], rxo.at[s, d], right)

    def xp_arrival(s, d):
        slot = lp if d == 0 else rp
        return rcopy(g.at[s, slot], g.at[s, slot], sxp.at[s, d], rxp.at[s, d], right)

    def f_copy(s, d):
        if d == 0:
            return rcopy(g.at[s, lo], g.at[s, lo], sf.at[s, 0], rf.at[s, 0], right)
        return rcopy(g.at[s, rp], g.at[s, rp], sf.at[s, 1], rf.at[s, 1], left)

    xf = (x + 2) % nx

    def f_arrival(s, d):
        slot = 2 * xf + yh if d == 0 else 2 * xf + 1 - yh
        return rcopy(g.at[s, slot], g.at[s, slot], sf.at[s, d], rf.at[s, d], right)

    def stage_own(s):
        y_copy(s).start()
        xo_copy(s, 0).start()
        xo_copy(s, 1).start()

    def stage_partner(s):
        y_arrival(s).wait_recv()
        xp_copy(s, 0).start()
        xp_copy(s, 1).start()

    def stage_far(s):
        xo_arrival(s, 0).wait_recv()
        f_copy(s, 0).start()
        xp_arrival(s, 1).wait_recv()
        f_copy(s, 1).start()

    def stage_finish(s):
        xo_arrival(s, 1).wait_recv()
        xp_arrival(s, 0).wait_recv()
        f_arrival(s, 0).wait_recv()
        f_arrival(s, 1).wait_recv()

    for s in range(nc):
        load_g(s).wait()
        if s < 3:
            stage_own(s)

    def m_copy(i):
        return rcopy(msg.at[t], msg.at[t], sm.at[i], rm.at[i], tensor_dev((t + i) % nt))

    def h1_copy(i):
        return rcopy(hr.at[t], hr.at[t], sh1.at[i], rh1.at[i], tensor_dev((t + i) % nt))

    load_a.wait()
    msg[t, :, nc * LANES :] = jnp.max(jnp.abs(acol[...].astype(jnp.float32)), axis=0, keepdims=True)
    for i in range(1, nt):
        m_copy(i).start()
    for i in range(1, nt):
        h1_copy(i).start()

    load_r.wait()
    block = 64

    def quant_grads(i, carry):
        at = pl.ds(pl.multiple_of(i * block, block), block)
        v = graw[at, :].astype(jnp.float32)
        gq[at, :] = jnp.clip(v * gscale, -QUANT_LIMIT, QUANT_LIMIT).astype(jnp.bfloat16)
        return jnp.maximum(carry, jnp.max(jnp.abs(v).reshape(block // 8, 8, width), axis=0))

    blocks = graw.shape[0] // block
    gpeak8 = lax.fori_loop(0, blocks // 2, quant_grads, jnp.zeros((8, width), jnp.float32))
    stage_partner(0)
    gpeak8 = lax.fori_loop(blocks // 2, blocks, quant_grads, gpeak8)
    gpeak = jnp.max(gpeak8, axis=0, keepdims=True)

    if nc > 1:
        stage_partner(1)
    stage_far(0)

    for i in range(1, nt):
        frm = (t + nt - i) % nt
        rcopy(msg.at[frm], msg.at[frm], sm.at[i], rm.at[i], partner_y).wait_recv()
    hmax = msg[0, :, : nc * LANES]
    apeak = msg[0, :, nc * LANES :]
    for i in range(1, nt):
        hmax = hmax + msg[i, :, : nc * LANES]
        apeak = jnp.maximum(apeak, msg[i, :, nc * LANES :])
    ascale = QUANT_LIMIT / jnp.maximum(hmax, SCALE_FLOOR)
    ascale_out[...] = ascale
    for k in range(nc):
        scales[k] = ascale[:, k * LANES : (k + 1) * LANES]
    ca = nc * LANES
    pv[:, :] = jnp.zeros(pv.shape, jnp.float32)
    pv[:, :ca] = apeak
    pv[:, ca : ca + width] = gpeak

    def r1_copy(s):
        return rcopy(s1.at[s], r1.at[s], sr1.at[s], rr1.at[s], other_core)

    def r2_copy(s):
        return rcopy(s2.at[s], r2.at[s], sr2.at[s], rr2.at[s], other_yl)

    def r3_copy(s, zo, zz):
        return rcopy(s3.at[s, zo], rb.at[z], sr3.at[s, zo], rr3.at[z], dp_dev(zz, yl, c))

    def compute(s):
        scale = scales[chunk(s)]
        for i in range(nt):
            v = g[s, i].astype(jnp.float32) * scale
            q[pl.ds(i * rows, rows), :] = jnp.clip(v, -QUANT_LIMIT, QUANT_LIMIT).astype(jnp.bfloat16)
        out = lax.dot_general(
            q[...], gq[...], (((0,), (0,)), ((), ())), preferred_element_type=jnp.float32
        )
        part[...] = out.reshape(8, 16, width)
        for i in range(4):
            s1[s, i] = part[2 * i + 1 - c].astype(jnp.bfloat16)

    def finish_r1(s):
        r1_copy(s).wait_recv()
        for zo in range(2):
            a = 2 * zo + 1 - yl
            b = 2 * zo + yl
            s2[s, zo] = (part[2 * a + c] + r1[s, a].astype(jnp.float32)).astype(jnp.bfloat16)
            keep2[zo] = part[2 * b + c] + r1[s, b].astype(jnp.float32)
        r2_copy(s).start()

    def finish_r2(s):
        r2_copy(s).wait_recv()
        k = chunk(s)
        for zo in range(2):
            s3[s, zo] = (keep2[zo] + r2[s, zo].astype(jnp.float32)).astype(jnp.bfloat16)
        for zo in range(2):
            zz = 2 * k + zo

            @pl.when(zz == z)
            def _():
                rb[z] = s3[s, zo]

            @pl.when(zz != z)
            def _():
                r3_copy(s, zo, zz).start()

    def p2_copy():
        return rcopy(pv, pcore, sp2, rp2, other_core)

    def p3_copy():
        return rcopy(pcore, pylo, sp3, rp3, other_yl)

    za, zb = z // pb, z % pb

    def p4_copy(i):
        return rcopy(
            pylo, pz1.at[i], sp4.at[i], rp4.at[i], dp_dev(za * pb + (zb + i) % pb, yl, c)
        )

    na = nz // pb

    def p5_copy(i):
        return rcopy(
            pz1.at[0], pz2.at[i], sp5.at[i], rp5.at[i], dp_dev(((za + i) % na) * pb + zb, yl, c)
        )

    def h3_copy(i):
        dst = ch.at[pl.ds(hrow, 8), pl.ds(hcol, LANES)]
        zz = (z // nc) * nc + (z % nc + i) % nc
        return rcopy(hb, dst, sh3.at[i], rh3.at[i], dp_dev(zz, yl, c))

    def h3_arrival(i):
        col = pl.multiple_of(((z % nc + nc - i) % nc) * LANES, LANES)
        dst = ch.at[pl.ds(hrow, 8), pl.ds(col, LANES)]
        return rcopy(hb, dst, sh3.at[i], rh3.at[i], other_core)

    def h4_copy():
        half = ch.at[pl.ds(hrow, 8), :]
        return rcopy(half, half, sh4, rh4, other_core)

    def h4_arrival():
        half = ch.at[pl.ds(pl.multiple_of(8 - hrow, 8), 8), :]
        return rcopy(half, half, sh4, rh4, other_core)

    def side_work(s):
        def h2():
            for i in range(1, nt):
                frm = (t + nt - i) % nt
                rcopy(hr.at[frm], hr.at[frm], sh1.at[i], rh1.at[i], partner_y).wait_recv()
            total = hr[0]
            for i in range(1, nt):
                total = total + hr[i]
            hb[...] = total
            ch[pl.ds(hrow, 8), pl.ds(hcol, LANES)] = total
            for i in range(1, nc):
                h3_copy(i).start()

        def p3():
            p2_copy().wait_recv()
            pcore[...] = jnp.maximum(pcore[...], pv[...])
            p3_copy().start()

        def p4():
            p3_copy().wait_recv()
            pylo[...] = jnp.maximum(pylo[...], pcore[...])
            for i in range(1, pb):
                p4_copy(i).start()

        def p5():
            m = pylo[...]
            for i in range(1, pb):
                p4_copy(i).wait_recv()
                m = jnp.maximum(m, pz1[i])
            pz1[0] = m
            for i in range(1, na):
                p5_copy(i).start()

        def p6():
            m = pz1[0]
            for i in range(1, na):
                p5_copy(i).wait_recv()
                m = jnp.maximum(m, pz2[i])
            peak_out[...] = m[:, :ca]
            gpeak_out[...] = m[:, ca : ca + width]

        def h4():
            for i in range(1, nc):
                h3_arrival(i).wait_recv()
            h4_copy().start()

        def h5():
            h4_arrival().wait_recv()
            hist_out[...] = ch[...]

        todo = [[p2_copy().start], [h2], [p3], [p4], [p5], [h4], [p6, h5]]
        for at, works in enumerate(todo):
            for work in works:
                pl.when(s == min(at, nc - 1))(work)

    def step(s, carry):
        @pl.when(s + 3 < nc)
        def _():
            stage_own(s + 3)

        @pl.when(s >= 1)
        def _():
            finish_r1(s - 1)

        @pl.when(s + 2 < nc)
        def _():
            stage_partner(s + 2)

        @pl.when(s + 1 < nc)
        def _():
            stage_far(s + 1)

        stage_finish(s)
        compute_into(s)
        r1_copy(s).start()

        @pl.when(s >= 1)
        def _():
            finish_r2(s - 1)

        side_work(s)
        return carry

    def compute_into(s):
        compute(s)

    lax.fori_loop(0, nc, step, 0)
    last = nc - 1
    finish_r1(last)
    finish_r2(last)

    total = rb[z].astype(jnp.float32)
    for i in range(1, nz):
        frm = (z + i) % nz
        rcopy(rb.at[frm], rb.at[frm], sr1.at[0], rr3.at[frm], other_core).wait_recv()
        total = total + rb[frm].astype(jnp.float32)
    sum_out[...] = total

    def drain(s, carry):
        y_copy(s).wait_send()
        for d in range(2):
            xo_copy(s, d).wait_send()
            xp_copy(s, d).wait_send()
            f_copy(s, d).wait_send()
        r1_copy(s).wait_send()
        r2_copy(s).wait_send()
        k = chunk(s)
        for zo in range(2):
            @pl.when(2 * k + zo != z)
            def _():
                r3_copy(s, zo, z).wait_send()
        return carry

    lax.fori_loop(0, nc, drain, 0)
    for i in range(1, nt):
        m_copy(i).wait_send()
        h1_copy(i).wait_send()
    for i in range(1, nc):
        h3_copy(i).wait_send()
    h4_copy().wait_send()
    p2_copy().wait_send()
    p3_copy().wait_send()
    for i in range(1, pb):
        p4_copy(i).wait_send()
    for i in range(1, na):
        p5_copy(i).wait_send()


def fused(acts, grads, ahist, ghist, owner, nz, nx):
    rows, model = acts.shape
    tokens, width = grads.shape
    nc, nt = nz // 2, 2 * nx
    na, pb = nz // 4, 4
    pw = model + -(-width // LANES) * LANES
    f32, bf16 = jnp.float32, jnp.bfloat16
    dma = pltpu.SemaphoreType.DMA
    vm = pltpu.VMEM
    scratch = [
        vm((nc, nt, rows, LANES), bf16),
        vm((rows, model), bf16),
        vm((tokens, width), bf16),
        vm((tokens, width), bf16),
        vm((tokens, LANES), bf16),
        vm((nc, 1, LANES), f32),
        vm((16, model), f32),
        vm((nt, 1, 2 * model), f32),
        vm((nt, 8, LANES), f32),
        vm((8, LANES), f32),
        vm((16, model), f32),
        vm((1, pw), f32),
        vm((1, pw), f32),
        vm((1, pw), f32),
        vm((pb, 1, pw), f32),
        vm((max(na, 2), 1, pw), f32),
        vm((8, 16, width), f32),
        vm((nc, 4, 16, width), bf16),
        vm((nc, 4, 16, width), bf16),
        vm((nc, 2, 16, width), bf16),
        vm((nc, 2, 16, width), bf16),
        vm((2, 16, width), f32),
        vm((nc, 2, 16, width), bf16),
        vm((nz, 16, width), bf16),
        dma((nc,)), dma, dma,
        dma((nc,)), dma((nc,)),
        dma((nc, 2)), dma((nc, 2)), dma((nc, 2)), dma((nc, 2)), dma((nc, 2)), dma((nc, 2)),
        dma((nt,)), dma((nt,)), dma((nt,)), dma((nt,)), dma((nc,)), dma((nc,)), dma, dma,
        dma, dma, dma, dma, dma((pb,)), dma((pb,)), dma((max(na, 2),)), dma((max(na, 2),)),
        dma((nc,)), dma((nc,)), dma((nc,)), dma((nc,)), dma((nc, 2)), dma((nz,)),
    ]
    vspec = pl.BlockSpec(memory_space=pltpu.VMEM)
    anyspec = pl.BlockSpec(memory_space=pl.ANY)
    return pl.pallas_call(
        functools.partial(kernel, nz, nx),
        out_shape=[
            jax.ShapeDtypeStruct((16, width), f32),
            jax.ShapeDtypeStruct((16, model), f32),
            jax.ShapeDtypeStruct((1, model), f32),
            jax.ShapeDtypeStruct((1, width), f32),
            jax.ShapeDtypeStruct((1, model), f32),
            jax.ShapeDtypeStruct((1, width), f32),
        ],
        in_specs=[anyspec, anyspec, vspec, vspec, vspec],
        out_specs=[vspec] * 6,
        scratch_shapes=scratch,
        compiler_params=pltpu.CompilerParams(
            collective_id=0, has_side_effects=True, vmem_limit_bytes=48 * 1024 * 1024
        ),
    )(acts, grads, ahist, ghist, owner)


def body(nz, nx, activations, gradients, act_history, grad_history, owner_rank, history_slot):
    model = act_history.shape[2]
    width = gradients.shape[1]
    my_rank = lax.axis_index("tensor")
    summed, current, act_peak, grad_peak, act_scale, grad_scale = fused(
        activations, gradients, act_history, grad_history, owner_rank.reshape(1, model), nz, nx
    )
    grad_factor = 1.0 / math.sqrt(gradients.shape[0] * lax.axis_size("dp"))
    row_base = lax.axis_index("dp") * 16
    row_scale = lax.dynamic_slice(act_scale, (0, row_base), (1, 16)).reshape(16, 1)
    weight_grad = summed / (row_scale * grad_scale) * grad_factor
    act_slots = history_slot[:model]
    grad_slots = lax.dynamic_slice_in_dim(history_slot, model + my_rank * width, width, 0)

    def place(history, peaks, slots):
        at = lax.broadcasted_iota(jnp.int32, history.shape, 0)
        return jnp.where(at == slots[None, :], peaks, history)

    act_history_out = place(current, act_peak, act_slots)[None]
    grad_history_out = place(grad_history, grad_peak, grad_slots)
    return (weight_grad, act_history_out, grad_history_out)


def solution(mesh):
    nz = mesh.shape["dp"] // 4
    nx = mesh.shape["tensor"] // 2
    placed = (
        P(("dp", "tensor"), None),
        P("dp", "tensor"),
        P("tensor", None, None),
        P(None, "tensor"),
        P(),
        P(),
    )
    return jax.shard_map(
        functools.partial(body, nz, nx),
        mesh=mesh,
        in_specs=placed,
        out_specs=(P("dp", "tensor"), P("tensor", None, None), P(None, "tensor")),
        check_vma=False,
    )
```

time: 253 us -> 76.5 us (0.30)
  the two profiles are of different devices: /device:TPU:8 before, /device:TPU:82 now
where the time goes in v1:
time: 76.5 us; the launch traced here: 76.2 us
  Pallas kernels  69.8 us (91%)
  local copies, waits for them, and re-layouts  4.37 us (6%)
  other arithmetic  1.37 us (2%)
    pallas_call x1, Pallas kernels, fused(): pl.pallas_call(functools.partial(kernel, nz, nx), out_shape=[jax.ShapeDty...  69.8 us
    unnamed x11, local copies, waits for them, and re-layouts  4.21 us

profile of v1, /device:TPU:82, one launch (start us, length us, event | category | flops | bytes accessed | tf_op | source)
XLA Modules:
  0.0 76.2 jit_solution(6309856649182641765)
XLA Ops:
  0.6 0.0 copy-start.2
  0.6 0.0 copy-start.1
  0.7 0.0 copy-start.3
  0.7 3.2 %copy.9.grads = bf16[2048,684]{1,0:T(8,128)(2,1)S(1)} copy(bf16[2048,684]{0,1:T(8,128)(2,1)} %param.7) | data formatting | bytes 5603328 | tf_op args[1]
  3.8 0.0 copy-done.2
  3.8 0.0 copy-done.1
  3.8 0.0 copy-done.3
  3.9 0.0 copy-start
  3.9 1.0 %copy-done = bf16[256,1024]{1,0:T(8,128)(2,1)S(1)} copy-done((bf16[256,1024]{1,0:T(8,128)(2,1)S(1)}, bf16[256,1024]{1,0:T(8,128)(2,1)}, u32[]{:S(2)}) %copy-start) | copy-done | bytes 524312
  4.9 0.0 copy-start.4
  4.9 0.0 slice-start
  4.9 69.8 %shard_map.85 = (f32[16,684]{1,0:T(8,128)S(1)}, f32[16,1024]{1,0:T(8,128)S(1)}, f32[1,1024]{1,0:T(1,128)S(1)}, f32[1,684]{1,0:T(1,128)S(1)}, f32[1,1024]{1,0:T(1,128)S(1)}, /*index=5*/f32[1,684]{1,0:T(1,128)S(1)}) custom-call(bf16[256,1024]{1,0:T(8,128)(2,1)S(1)} %copy-done, bf16[2048,684]{1,0:T(8,128)(2,1)S(1)} %copy.9.grads, f32[1,16,1024]{2,1,0:T(8,128)S(1)} %copy-done.2, ...), custom_call_target="tpu_custom_call" | custom-call | tf_op jit(solution)/shard_map/pallas_call | solution.py:459
  74.7 0.1 dynamic-slice_bitcast_fusion
  74.8 0.0 copy-done.4
  74.8 0.1 dynamic_slice.7
  74.9 0.7 divide_multiply_fusion
  75.6 0.0 slice-done
  75.6 0.6 select_bitcast_fusion
  (2 shorter events, 0.0 us)
Async XLA Ops:
  0.6 3.2 %copy-start.2 = (f32[1,16,1024]{2,1,0:T(8,128)S(1)}, f32[1,16,1024]{2,1,0:T(8,128)}, u32[]{:S(2)}) copy-start(f32[1,16,1024]{2,1,0:T(8,128)} %ahist.1) | copy-start | bytes 196612
  0.6 3.2 %copy-start.1 = (f32[16,684]{1,0:T(8,128)S(1)}, f32[16,684]{1,0:T(8,128)}, u32[]{:S(2)}) copy-start(f32[16,684]{1,0:T(8,128)} %ghist.1) | copy-start | bytes 131332
  0.7 3.2 %copy-start.3 = (s32[1024]{0:T(1024)S(1)}, s32[1024]{0:T(1024)}, u32[]{:S(2)}) copy-start(s32[1024]{0:T(1024)} %param.10) | copy-start | bytes 12292
  3.9 1.0 %copy-start = (bf16[256,1024]{1,0:T(8,128)(2,1)S(1)}, bf16[256,1024]{1,0:T(8,128)(2,1)}, u32[]{:S(2)}) copy-start(bf16[256,1024]{1,0:T(8,128)(2,1)} %acts.1) | copy-start | bytes 1572868
  4.9 69.9 %copy-start.4 = (s32[6496]{0:T(1024)S(1)}, s32[6496]{0:T(1024)}, u32[]{:S(2)}) copy-start(s32[6496]{0:T(1024)} %param.11) | copy-start | bytes 77956
  4.9 70.7 %slice-start = ((s32[6496]{0:T(1024)}), s32[1024]{0:T(1024)S(1)}, s32[]{:S(2)}) async-start(s32[6496]{0:T(1024)} %param.11), calls=%async_computation | async-start | bytes 8192 | tf_op jit(solution)/shard_map/slice | solution.py:489

commit v2 on v1

v2 whole, which is shorter than its diff:
```python
import functools
import math

import jax
import jax.numpy as jnp
from jax import lax
from jax.experimental import pallas as pl
from jax.experimental.pallas import tpu as pltpu
from jax.sharding import PartitionSpec as P

QUANT_LIMIT = 448.0
SCALE_FLOOR = 0.25
LANES = 128
BLOCK = 64
MESH = pl.DeviceIdType.MESH


def kernel(
    nz, nx, acts, grads, ahist, ghist, owner,
    sum_out, hist_out, peak_out, gpeak_out, ascale_out, gscale_out,
    g, acol, graw, gq, q, ah, gh, ow, gcol, gpk, scales, mh, small, hb, ch,
    pv, pcore, pylo, pzz, pfar,
    part, s1, r1, s2, r2, keep2, s3, r3, keep3, s4, rb, own_sum,
    ld_g, ld_x,
    sy, ry, sxo, rxo, sxp, rxp, sf, rf, sy2, ry2,
    sh3, rh3, sh4, rh4, sp2, rp2, sp3, rp3, sp4, rp4, sp5, rp5,
    sr1, rr1, sr2, rr2, sr3, rr3, sr4, rr4, tok1, tok2,
):
    nc = nz // 2
    nt = 2 * nx
    early = max(3 * nc // 8, 1)
    tok_step = min(3, nc - 1)
    rows = acts.shape[0]
    width, tokens = grads.shape
    wp = gq.shape[0]
    t = lax.axis_index("tensor")
    dpi = lax.axis_index("dp")
    x, yh = t // 2, t % 2
    z, yl, c = dpi // 4, (dpi // 2) % 2, dpi % 2
    zp, zq = z // 2, z % 2
    xr, xl, xf = (x + 1) % nx, (x + nx - 1) % nx, (x + 2) % nx
    yo = 1 - yh

    def tensor_dev(tt):
        return {"dp": dpi, "tensor": tt}

    def dp_dev(zz, yy, cc):
        return {"dp": zz * 4 + yy * 2 + cc, "tensor": t}

    def pair_dev(pp):
        return dp_dev(2 * pp + zq, yl, c)

    def rcopy(src, dst, ss, rs, device):
        return pltpu.make_async_remote_copy(
            src_ref=src, dst_ref=dst, send_sem=ss, recv_sem=rs,
            device_id=device, device_id_type=MESH,
        )

    def signal(sem, device):
        pl.semaphore_signal(sem, inc=1, device_id=device, device_id_type=MESH)

    def chunk(s):
        half = (s + 1) // 2
        return (zp + nc // 2 + (1 - 2 * (s % 2)) * half + 2 * nc) % nc

    partner_y = tensor_dev(2 * x + yo)
    right = tensor_dev(2 * xr + yh)
    left = tensor_dev(2 * xl + yh)
    other_core = dp_dev(z, yl, 1 - c)
    other_yl = dp_dev(z, 1 - yl, c)
    other_z = dp_dev(2 * zp + 1 - zq, yl, c)

    def load_g(s):
        col = pl.multiple_of(chunk(s) * LANES, LANES)
        return pltpu.make_async_copy(acts.at[:, pl.ds(col, LANES)], g.at[s, t], ld_g.at[s])

    loads = [
        pltpu.make_async_copy(src, dst, ld_x.at[i])
        for i, (src, dst) in enumerate(
            [(ahist, ah), (owner, ow), (ghist, gh), (acts, acol), (grads, graw)]
        )
    ]
    loads[0].start()
    loads[1].start()
    for s in range(nc):
        load_g(s).start()
    for i in (3, 2, 4):
        loads[i].start()

    bar = pltpu.get_barrier_semaphore()
    for device in (partner_y, right, left, other_core, other_yl, other_z):
        signal(bar, device)
    for i in range(1, nc):
        @pl.when(jnp.logical_and(zp < early, zp + i < nc))
        def _():
            signal(bar, pair_dev(zp + i))

    def to_rows(vec, at, count):
        for k in range(count):
            small[t, at + k : at + k + 1, :] = vec[:, k * LANES : (k + 1) * LANES]

    loads[0].wait()
    loads[1].wait()
    held = jnp.where(ow[...] == t, ah[0], jnp.float32(0.0))
    mh[...] = held
    to_rows(jnp.max(held, axis=0, keepdims=True), 0, nc)
    hcol = pl.multiple_of(zp * LANES, LANES)
    hrow = pl.multiple_of(c * 8, 8)
    small[t, 8:16, :] = mh[pl.ds(hrow, 8), pl.ds(hcol, LANES)]
    loads[3].wait()
    to_rows(jnp.max(jnp.abs(acol[...].astype(jnp.float32)), axis=0, keepdims=True), 16, nc)

    pl.semaphore_wait(bar, 6 + jnp.minimum(zp, early))
    for i in range(early):
        @pl.when(i < zp)
        def _():
            signal(tok1, pair_dev(i))

    def at_slot(s, xx, yy):
        if isinstance(s, int) and s == nc:
            return small.at[2 * xx + yy]
        return g.at[s, 2 * xx + yy]

    def y_copy(s):
        return rcopy(at_slot(s, x, yh), at_slot(s, x, yh), sy.at[s], ry.at[s], partner_y)

    def y_arrival(s):
        return rcopy(at_slot(s, x, yo), at_slot(s, x, yo), sy.at[s], ry.at[s], partner_y)

    def xo_copy(s, d):
        a = at_slot(s, x, yh)
        return rcopy(a, a, sxo.at[s, d], rxo.at[s, d], right if d == 0 else left)

    def xo_arrival(s, d):
        a = at_slot(s, xl if d == 0 else xr, yh)
        return rcopy(a, a, sxo.at[s, d], rxo.at[s, d], right)

    def xp_copy(s, d):
        a = at_slot(s, x, yo)
        return rcopy(a, a, sxp.at[s, d], rxp.at[s, d], right if d == 0 else left)

    def xp_arrival(s, d):
        a = at_slot(s, xl if d == 0 else xr, yo)
        return rcopy(a, a, sxp.at[s, d], rxp.at[s, d], right)

    def far_own(s, d):
        a = at_slot(s, xl if d == 0 else xr, yh)
        return rcopy(a, a, sf.at[s, 0], rf.at[s, 0], right if d == 0 else left)

    def far_own_arrival(s):
        a = at_slot(s, xf, yh)
        return rcopy(a, a, sf.at[s, 0], rf.at[s, 0], right)

    def far_other(s, d):
        a = at_slot(s, xl if d == 0 else xr, yo)
        return rcopy(a, a, sf.at[s, 1], rf.at[s, 1], right if d == 0 else left)

    def far_other_arrival(s):
        a = at_slot(s, xf, yo)
        return rcopy(a, a, sf.at[s, 1], rf.at[s, 1], right)

    def y2_copy(s):
        a = at_slot(s, xf, yh)
        return rcopy(a, a, sy2.at[s], ry2.at[s], partner_y)

    def y2_arrival(s):
        a = at_slot(s, xf, yo)
        return rcopy(a, a, sy2.at[s], ry2.at[s], partner_y)

    def cond(pred, work):
        if isinstance(pred, bool):
            if pred:
                work()
        else:
            pl.when(pred)(work)

    def kind_a(s):
        if isinstance(s, int) and s == nc:
            return True
        return s % 7 == 0

    def kind_c(s):
        if isinstance(s, int) and s == nc:
            return False
        return s % 7 != 0

    def stage_own(s):
        y_copy(s).start()
        xo_copy(s, 0).start()
        xo_copy(s, 1).start()

    def stage_partner(s):
        y_arrival(s).wait_recv()
        xp_copy(s, 0).start()
        xp_copy(s, 1).start()

    def stage_far_own(s):
        def go(d):
            xo_arrival(s, d).wait_recv()
            far_own(s, d).start()

        cond(s % 2 == 0, lambda: go(0))
        cond(s % 2 == 1, lambda: go(1))

    def stage_far_other(s):
        def kind_a_work():
            def go(d):
                xp_arrival(s, d).wait_recv()
                far_other(s, d).start()

            cond(s % 2 == 0, lambda: go(1))
            cond(s % 2 == 1, lambda: go(0))

        def kind_c_work():
            far_own_arrival(s).wait_recv()
            y2_copy(s).start()

        cond(kind_a(s), kind_a_work)
        cond(kind_c(s), kind_c_work)

    def stage_finish(s):
        def even():
            xo_arrival(s, 1).wait_recv()

        def odd():
            xo_arrival(s, 0).wait_recv()

        cond(s % 2 == 0, even)
        cond(s % 2 == 1, odd)

        def kind_a_work():
            cond(s % 2 == 0, lambda: xp_arrival(s, 0).wait_recv())
            cond(s % 2 == 1, lambda: xp_arrival(s, 1).wait_recv())
            far_own_arrival(s).wait_recv()
            far_other_arrival(s).wait_recv()

        def kind_c_work():
            xp_arrival(s, 0).wait_recv()
            xp_arrival(s, 1).wait_recv()
            y2_arrival(s).wait_recv()

        cond(kind_a(s), kind_a_work)
        cond(kind_c(s), kind_c_work)

    stage_own(nc)
    for s in range(nc):
        load_g(s).wait()
        if s < 3:
            stage_own(s)

    loads[2].wait()
    gscale = QUANT_LIMIT / jnp.maximum(jnp.max(gh[...], axis=0, keepdims=True), SCALE_FLOOR)
    gscale_out[...] = gscale
    pad = jnp.zeros((1, wp - width), jnp.float32)
    gcol[...] = jnp.broadcast_to(jnp.concatenate([gscale, pad], axis=1), (LANES, wp)).T
    loads[4].wait()

    def quant_rows(at, count):
        scale = gcol[at, :]
        top = jnp.zeros((count, LANES), jnp.float32)
        for j in range(tokens // LANES):
            v = graw[at, j * LANES : (j + 1) * LANES].astype(jnp.float32)
            gq[at, j * LANES : (j + 1) * LANES] = jnp.clip(
                v * scale, -QUANT_LIMIT, QUANT_LIMIT
            ).astype(jnp.bfloat16)
            top = jnp.maximum(top, jnp.abs(v))
        gpk[at, :] = top

    def quant_block(i, carry):
        quant_rows(pl.ds(pl.multiple_of(i * BLOCK, BLOCK), BLOCK), BLOCK)
        return carry

    full = width // BLOCK
    lax.fori_loop(0, full // 3, quant_block, 0)
    stage_partner(nc)
    stage_partner(0)
    stage_far_own(nc)
    stage_far_own(0)
    lax.fori_loop(full // 3, 2 * full // 3, quant_block, 0)
    if nc > 1:
        stage_partner(1)
        stage_far_own(1)
    stage_far_other(nc)
    stage_far_other(0)
    lax.fori_loop(2 * full // 3, full, quant_block, 0)
    if width > full * BLOCK:
        quant_rows(slice(full * BLOCK, width), width - full * BLOCK)
    gq[width:, :] = jnp.zeros((wp - width, tokens), jnp.bfloat16)
    gpk[width:, :] = jnp.zeros((wp - width, LANES), jnp.float32)
    gpeak = jnp.max(gpk[...].T, axis=0, keepdims=True)

    stage_finish(nc)
    total_small = small[0]
    apeak = small[0, 16:24, :]
    for i in range(1, nt):
        total_small = total_small + small[i]
        apeak = jnp.maximum(apeak, small[i, 16:24, :])
    ascale = QUANT_LIMIT / jnp.maximum(total_small[0:8, :], SCALE_FLOOR)
    for k in range(nc):
        scales[k] = ascale[k : k + 1, :]
        ascale_out[:, k * LANES : (k + 1) * LANES] = ascale[k : k + 1, :]
    hb[...] = total_small[8:16, :]
    ch[pl.ds(hrow, 8), pl.ds(hcol, LANES)] = total_small[8:16, :]
    pv[0:8, :] = apeak
    for k in range(wp // LANES):
        pv[8 + k : 9 + k, :] = gpeak[:, k * LANES : (k + 1) * LANES]
    pv[8 + wp // LANES :, :] = jnp.zeros((8 - wp // LANES, LANES), jnp.float32)

    def r1_copy(s):
        return rcopy(s1.at[s], r1.at[s], sr1.at[s], rr1.at[s], other_core)

    def r2_copy(s):
        return rcopy(s2.at[s], r2.at[s], sr2.at[s], rr2.at[s], other_yl)

    def r3_copy(s):
        return rcopy(s3.at[s], r3.at[s], sr3.at[s], rr3.at[s], other_z)

    def r4_copy(s):
        return rcopy(s4.at[s], rb.at[zp], sr4.at[s], rr4.at[zp], pair_dev(chunk(s)))

    def compute(s):
        scale = scales[chunk(s)]
        for i in range(nt):
            v = g[s, i].astype(jnp.float32) * scale
            q[pl.ds(i * rows, rows), :] = jnp.clip(v, -QUANT_LIMIT, QUANT_LIMIT).astype(jnp.bfloat16)
        out = jnp.dot(gq[...], q[...], preferred_element_type=jnp.float32)
        part[...] = out.T.reshape(8, 16, wp)
        for i in range(4):
            s1[s, i] = part[2 * i + 1 - c].astype(jnp.bfloat16)

    def finish_r1(s):
        r1_copy(s).wait_recv()
        for zo in range(2):
            a = 2 * zo + 1 - yl
            b = 2 * zo + yl
            s2[s, zo] = (part[2 * a + c] + r1[s, a].astype(jnp.float32)).astype(jnp.bfloat16)
            keep2[zo] = part[2 * b + c] + r1[s, b].astype(jnp.float32)
        r2_copy(s).start()

    def finish_r2(s):
        r2_copy(s).wait_recv()
        s3[s] = (keep2[1 - zq] + r2[s, 1 - zq].astype(jnp.float32)).astype(jnp.bfloat16)
        keep3[s] = keep2[zq] + r2[s, zq].astype(jnp.float32)
        r3_copy(s).start()

    def finish_r3(s):
        r3_copy(s).wait_recv()
        total = keep3[s] + r3[s].astype(jnp.float32)
        s4[s] = total.astype(jnp.bfloat16)
        own_sum[...] = total

    def start_r4(s):
        @pl.when(chunk(s) != zp)
        def _():
            r4_copy(s).start()

    def p2_copy():
        return rcopy(pv, pcore, sp2, rp2, other_core)

    def p3_copy():
        return rcopy(pcore, pylo, sp3, rp3, other_yl)

    def p4_copy():
        return rcopy(pylo, pzz, sp4, rp4, other_z)

    def p5_copy(i):
        return rcopy(pzz, pfar.at[i], sp5.at[i], rp5.at[i], pair_dev((zp + i) % nc))

    def h3_copy(i):
        dst = ch.at[pl.ds(hrow, 8), pl.ds(hcol, LANES)]
        return rcopy(hb, dst, sh3.at[i], rh3.at[i], pair_dev((zp + i) % nc))

    def h3_arrival(i):
        col = pl.multiple_of(((zp + nc - i) % nc) * LANES, LANES)
        dst = ch.at[pl.ds(hrow, 8), pl.ds(col, LANES)]
        return rcopy(hb, dst, sh3.at[i], rh3.at[i], other_core)

    def h4_copy():
        half = ch.at[pl.ds(hrow, 8), :]
        return rcopy(half, half, sh4, rh4, other_core)

    def h4_arrival():
        half = ch.at[pl.ds(pl.multiple_of(8 - hrow, 8), 8), :]
        return rcopy(half, half, sh4, rh4, other_core)

    def side_work(s):
        def p3():
            p2_copy().wait_recv()
            pcore[...] = jnp.maximum(pcore[...], pv[...])
            p3_copy().start()

        def p4():
            p3_copy().wait_recv()
            pylo[...] = jnp.maximum(pylo[...], pcore[...])
            p4_copy().start()

        def far():
            p4_copy().wait_recv()
            pzz[...] = jnp.maximum(pzz[...], pylo[...])
            for i in range(1, nc):
                h3_copy(i).start()
            for i in range(1, nc):
                p5_copy(i).start()

        def h4():
            for i in range(1, nc):
                h3_arrival(i).wait_recv()
            h4_copy().start()

        todo = [(0, p2_copy().start), (1, p3), (2, p4), (tok_step + 1, far), (6, h4)]
        for at, work in todo:
            pl.when(s == min(at, nc - 1))(work)

    def tokens_wait():
        @pl.when(zp < early)
        def _():
            pl.semaphore_wait(tok1, nc - 1 - zp)
            for pp in range(early, nc):
                @pl.when((nc - 1 - pp) % early == zp)
                def _():
                    signal(tok2, pair_dev(pp))

        @pl.when(zp >= early)
        def _():
            pl.semaphore_wait(tok2, 1)

    def step(s, carry):
        @pl.when(s + 3 < nc)
        def _():
            stage_own(s + 3)

        @pl.when(s >= 1)
        def _():
            finish_r1(s - 1)

        @pl.when(s + 2 < nc)
        def _():
            stage_partner(s + 2)
            stage_far_own(s + 2)

        @pl.when(s + 1 < nc)
        def _():
            stage_far_other(s + 1)

        @pl.when(s >= 2)
        def _():
            finish_r3(s - 2)

        @pl.when(s == tok_step)
        def _():
            tokens_wait()
            for i in range(max(tok_step - 2, 0)):
                start_r4(i)

        @pl.when(jnp.logical_and(s >= tok_step, s >= 2))
        def _():
            start_r4(s - 2)

        stage_finish(s)
        compute(s)
        r1_copy(s).start()

        @pl.when(s >= 1)
        def _():
            finish_r2(s - 1)

        side_work(s)
        return carry

    lax.fori_loop(0, nc, step, 0)
    last = nc - 1
    finish_r1(last)
    if nc > 1:
        finish_r3(last - 1)
        start_r4(last - 1)
    h4_arrival().wait_recv()
    hist_out[...] = ch[...]
    finish_r2(last)
    top = pzz[...]
    for i in range(1, nc):
        p5_copy(i).wait_recv()
        top = jnp.maximum(top, pfar[i])
    for k in range(nc):
        peak_out[:, k * LANES : (k + 1) * LANES] = top[k : k + 1, :]
    for k in range(wp // LANES):
        n = min(width - k * LANES, LANES)
        gpeak_out[:, k * LANES : k * LANES + n] = top[8 + k : 9 + k, :n]
    finish_r3(last)

    total = own_sum[...]
    for i in range(1, nc):
        frm = (zp + i) % nc
        rcopy(rb.at[frm], rb.at[frm], sr4.at[0], rr4.at[frm], other_core).wait_recv()
        total = total + rb[frm].astype(jnp.float32)
    sum_out[...] = total[:, :width]

    def drain_gather(s):
        y_copy(s).wait_send()
        for d in range(2):
            xo_copy(s, d).wait_send()
            xp_copy(s, d).wait_send()
        far_own(s, 0).wait_send()
        cond(kind_a(s), lambda: far_other(s, 0).wait_send())
        cond(kind_c(s), lambda: y2_copy(s).wait_send())

    def drain(s, carry):
        drain_gather(s)
        r1_copy(s).wait_send()
        r2_copy(s).wait_send()
        r3_copy(s).wait_send()

        @pl.when(chunk(s) != zp)
        def _():
            r4_copy(s).wait_send()

        return carry

    drain_gather(nc)
    lax.fori_loop(0, nc, drain, 0)
    h4_copy().wait_send()
    p2_copy().wait_send()
    p3_copy().wait_send()
    p4_copy().wait_send()
    for i in range(1, nc):
        h3_copy(i).wait_send()
        p5_copy(i).wait_send()


def fused(acts, grads, ahist, ghist, owner, nz, nx):
    rows, model = acts.shape
    width, tokens = grads.shape
    nc, nt = nz // 2, 2 * nx
    wp = -(-width // LANES) * LANES
    f32, bf16 = jnp.float32, jnp.bfloat16
    dma = pltpu.SemaphoreType.DMA
    vm = pltpu.VMEM
    scratch = [
        vm((nc, nt, rows, LANES), bf16),
        vm((rows, model), bf16),
        vm((width, tokens), bf16),
        vm((wp, tokens), bf16),
        vm((tokens, LANES), bf16),
        vm((1, 16, model), f32),
        vm((16, width), f32),
        vm((1, model), jnp.int32),
        vm((wp, LANES), f32),
        vm((wp, LANES), f32),
        vm((nc, 1, LANES), f32),
        vm((16, model), f32),
        vm((nt, 24, LANES), f32),
        vm((8, LANES), f32),
        vm((16, model), f32),
        vm((16, LANES), f32),
        vm((16, LANES), f32),
        vm((16, LANES), f32),
        vm((16, LANES), f32),
        vm((nc, 16, LANES), f32),
        vm((8, 16, wp), f32),
        vm((nc, 4, 16, wp), bf16),
        vm((nc, 4, 16, wp), bf16),
        vm((nc, 2, 16, wp), bf16),
        vm((nc, 2, 16, wp), bf16),
        vm((2, 16, wp), f32),
        vm((nc, 16, wp), bf16),
        vm((nc, 16, wp), bf16),
        vm((nc, 16, wp), f32),
        vm((nc, 16, wp), bf16),
        vm((nc, 16, wp), bf16),
        vm((16, wp), f32),
        dma((nc,)), dma((5,)),
        dma((nc + 1,)), dma((nc + 1,)),
        dma((nc + 1, 2)), dma((nc + 1, 2)), dma((nc + 1, 2)), dma((nc + 1, 2)),
        dma((nc + 1, 2)), dma((nc + 1, 2)), dma((nc + 1,)), dma((nc + 1,)),
        dma((nc,)), dma((nc,)), dma, dma,
        dma, dma, dma, dma, dma, dma, dma((nc,)), dma((nc,)),
        dma((nc,)), dma((nc,)), dma((nc,)), dma((nc,)),
        dma((nc,)), dma((nc,)), dma((nc,)), dma((nc,)),
        pltpu.SemaphoreType.REGULAR, pltpu.SemaphoreType.REGULAR,
    ]
    vspec = pl.BlockSpec(memory_space=pltpu.VMEM)
    anyspec = pl.BlockSpec(memory_space=pl.ANY)
    return pl.pallas_call(
        functools.partial(kernel, nz, nx),
        out_shape=[
            jax.ShapeDtypeStruct((16, width), f32),
            jax.ShapeDtypeStruct((16, model), f32),
            jax.ShapeDtypeStruct((1, model), f32),
            jax.ShapeDtypeStruct((1, width), f32),
            jax.ShapeDtypeStruct((1, model), f32),
            jax.ShapeDtypeStruct((1, width), f32),
        ],
        in_specs=[anyspec] * 5,
        out_specs=[vspec] * 6,
        scratch_shapes=scratch,
        compiler_params=pltpu.CompilerParams(
            collective_id=0, has_side_effects=True, vmem_limit_bytes=60 * 1024 * 1024
        ),
    )(acts, grads, ahist, ghist, owner)


def body(nz, nx, activations, gradients, act_history, grad_history, owner_rank, history_slot):
    model = act_history.shape[2]
    width = gradients.shape[1]
    my_rank = lax.axis_index("tensor")
    summed, current, act_peak, grad_peak, act_scale, grad_scale = fused(
        activations, gradients.T, act_history, grad_history, owner_rank.reshape(1, model), nz, nx
    )
    grad_factor = 1.0 / math.sqrt(gradients.shape[0] * lax.axis_size("dp"))
    row_base = lax.axis_index("dp") * 16
    row_scale = lax.dynamic_slice(act_scale, (0, row_base), (1, 16)).reshape(16, 1)
    weight_grad = summed / (row_scale * grad_scale) * grad_factor
    act_slots = history_slot[:model]
    grad_slots = lax.dynamic_slice_in_dim(history_slot, model + my_rank * width, width, 0)

    def place(history, peaks, slots):
        at = lax.broadcasted_iota(jnp.int32, history.shape, 0)
        return jnp.where(at == slots[None, :], peaks, history)

    act_history_out = place(current, act_peak, act_slots)[None]
    grad_history_out = place(grad_history, grad_peak, grad_slots)
    return (weight_grad, act_history_out, grad_history_out)


def solution(mesh):
    nz = mesh.shape["dp"] // 4
    nx = mesh.shape["tensor"] // 2
    placed = (
        P(("dp", "tensor"), None),
        P("dp", "tensor"),
        P("tensor", None, None),
        P(None, "tensor"),
        P(),
        P(),
    )
    return jax.shard_map(
        functools.partial(body, nz, nx),
        mesh=mesh,
        in_specs=placed,
        out_specs=(P("dp", "tensor"), P("tensor", None, None), P(None, "tensor")),
        check_vma=False,
    )
```

time: 76.5 us -> 76.6 us (level)
  the two profiles are of different devices: /device:TPU:82 before, /device:TPU:4 now
where the time goes in v2:
time: 76.6 us; the launch traced here: 76.3 us
  Pallas kernels  69.8 us (91%)
  other arithmetic  4.35 us (6%)
  local copies, waits for them, and re-layouts  1.47 us (2%)
    pallas_call x1, Pallas kernels, fused(): pl.pallas_call(functools.partial(kernel, nz, nx), out_shape=[jax.ShapeDty...  69.8 us

profile of v2, /device:TPU:4, one launch (start us, length us, event | category | flops | bytes accessed | tf_op | source)
XLA Modules:
  0.0 76.3 jit_solution(17839156005658760821)
XLA Ops:
  0.6 0.0 slice-start
  0.6 0.0 copy-start
  0.7 0.8 %dynamic_slice.7 = s32[684]{0:T(1024)S(1)} dynamic-slice(s32[6496]{0:T(1024)} %param.11, s32[]{:T(128)S(6)} %select_n.16), dynamic_slice_sizes={684} | dynamic-slice | bytes 5476 | tf_op jit(solution)/shard_map/dynamic_slice | solution.py:613
  1.4 69.8 %shard_map.85 = (f32[16,684]{1,0:T(8,128)}, f32[16,1024]{1,0:T(8,128)}, f32[1,1024]{1,0:T(1,128)}, f32[1,684]{1,0:T(1,128)}, f32[1,1024]{1,0:T(1,128)}, /*index=5*/f32[1,684]{1,0:T(1,128)}) custom-call(bf16[256,1024]{1,0:T(8,128)(2,1)} %acts.1, bf16[684,2048]{1,0:T(8,128)(2,1)} %bitcast.7, f32[1,16,1024]{2,1,0:T(8,128)} %ahist.1, f32[16,684]{1,0:T(8,128)} %ghist.1, ...), custom_call_target="tpu_custom_call" | custom-call | tf_op jit(solution)/shard_map/pallas_call | solution.py:582
  71.2 0.7 dynamic-slice_bitcast_fusion
  71.9 0.7 reduce
  72.6 0.7 reduce.1
  73.3 0.0 copy-done
  73.3 1.5 %divide_multiply_fusion = (f32[16,684]{1,0:T(8,128)}, f32[16,684]{1,0:T(8,128)}) fusion(f32[16,684]{1,0:T(8,128)} %get-tuple-element.9, f32[684]{0:T(1024)S(1)} %reduce, f32[16]{0:T(128)S(1)} %dynamic-slice_bitcast_fusion, f32[16,684]{1,0:T(8,128)S(1)} %copy-done, f32[684]{0:T(1024)S(1)} %reduce.1, s32[684]{0:T(1024)S(1)} %dynamic_slice.7), kind=kLoop, calls=%fused_computation.3 | loop fusion | flops 54720 | bytes 183376 | tf_op jit(solution)/shard_map/mul | solution.py:611
  74.8 0.0 slice-done
  74.8 1.5 %select_bitcast_fusion = f32[1,16,1024]{2,1,0:T(8,128)} fusion(f32[16,1024]{1,0:T(8,128)} %get-tuple-element.13, f32[1024]{0:T(1024)} %bitcast.9, s32[1024]{0:T(1024)S(1)} %slice-done), kind=kLoop, calls=%fused_computation | loop fusion | flops 32768 | bytes 139264 | tf_op jit(solution)/shard_map/broadcast_in_dim | solution.py:619
Async XLA Ops:
  0.6 74.2 %slice-start = ((s32[6496]{0:T(1024)}), s32[1024]{0:T(1024)S(1)}, s32[]{:S(2)}) async-start(s32[6496]{0:T(1024)} %param.11), calls=%async_computation | async-start | bytes 8192 | tf_op jit(solution)/shard_map/slice | solution.py:612
  0.6 72.7 %copy-start = (f32[16,684]{1,0:T(8,128)S(1)}, f32[16,684]{1,0:T(8,128)}, u32[]{:S(2)}) copy-start(f32[16,684]{1,0:T(8,128)} %ghist.1) | copy-start | bytes 131332

commit v3 on v2

--- a/solution.py
+++ b/solution.py
@@ -12,24 +12,27 @@
 SCALE_FLOOR = 0.25
 LANES = 128
 BLOCK = 64
+AHEAD = 4
+DIRECT = 1
 MESH = pl.DeviceIdType.MESH
 
 
 def kernel(
-    nz, nx, acts, grads, ahist, ghist, owner,
-    sum_out, hist_out, peak_out, gpeak_out, ascale_out, gscale_out,
-    g, acol, graw, gq, q, ah, gh, ow, gcol, gpk, scales, mh, small, hb, ch,
+    nz, nx, factor, acts, grads, ahist, ghist, owner, slots,
+    wgrad_out, hist_out, ghist_out,
+    g, acol, graw, gq, q, ah, gh, ow, sl, gsl, peak_row, gpeak_row, gcol, gpk, scales, mh, small, hb, ch,
     pv, pcore, pylo, pzz, pfar,
-    part, s1, r1, s2, r2, keep2, s3, r3, keep3, s4, rb, own_sum,
+    part, s1, r1, s2, r2, keep2, s4, rb, own_sum, sd, rd, keepd,
     ld_g, ld_x,
     sy, ry, sxo, rxo, sxp, rxp, sf, rf, sy2, ry2,
     sh3, rh3, sh4, rh4, sp2, rp2, sp3, rp3, sp4, rp4, sp5, rp5,
-    sr1, rr1, sr2, rr2, sr3, rr3, sr4, rr4, tok1, tok2,
+    sr1, rr1, sr2, rr2, sr4, rr4, srd, rrd, tok1, tok2,
 ):
     nc = nz // 2
     nt = 2 * nx
     early = max(3 * nc // 8, 1)
-    tok_step = min(3, nc - 1)
+    tok_step = min(1, nc - 1)
+    chain = nc - min(DIRECT, nc)
     rows = acts.shape[0]
     width, tokens = grads.shape
     wp = gq.shape[0]
@@ -60,8 +63,13 @@
         pl.semaphore_signal(sem, inc=1, device_id=device, device_id_type=MESH)
 
     def chunk(s):
-        half = (s + 1) // 2
-        return (zp + nc // 2 + (1 - 2 * (s % 2)) * half + 2 * nc) % nc
+        hf = nc // 2
+        late = s // hf
+        j = 2 * hf - 1 - s
+        high = zp // hf
+        u = high * (zp - hf) + (1 - high) * (hf - 1 - zp)
+        flip = (u + j) % 2 + 2 * ((u // 2 + j // 2) % 2)
+        return (1 - late) * s + late * (hf + flip % hf)
 
     partner_y = tensor_dev(2 * x + yo)
     right = tensor_dev(2 * xr + yh)
@@ -70,6 +78,13 @@
     other_yl = dp_dev(z, 1 - yl, c)
     other_z = dp_dev(2 * zp + 1 - zq, yl, c)
 
+    def cube_index(i):
+        return (zq + i // 4) % 2, (yl + i // 2 % 2) % 2, (c + i % 2) % 2
+
+    def cube_dev(i):
+        zz, yy, cc = cube_index(i)
+        return dp_dev(2 * zp + zz, yy, cc)
+
     def load_g(s):
         col = pl.multiple_of(chunk(s) * LANES, LANES)
         return pltpu.make_async_copy(acts.at[:, pl.ds(col, LANES)], g.at[s, t], ld_g.at[s])
@@ -77,19 +92,21 @@
     loads = [
         pltpu.make_async_copy(src, dst, ld_x.at[i])
         for i, (src, dst) in enumerate(
-            [(ahist, ah), (owner, ow), (ghist, gh), (acts, acol), (grads, graw)]
+            [(ahist, ah), (owner, ow), (ghist, gh), (acts, acol), (grads, graw), (slots, sl)]
         )
     ]
     loads[0].start()
     loads[1].start()
     for s in range(nc):
         load_g(s).start()
-    for i in (3, 2, 4):
+    for i in (3, 2, 4, 5):
         loads[i].start()
 
     bar = pltpu.get_barrier_semaphore()
-    for device in (partner_y, right, left, other_core, other_yl, other_z):
+    for device in (partner_y, right, left):
         signal(bar, device)
+    for i in range(1, 8):
+        signal(bar, cube_dev(i))
     for i in range(1, nc):
         @pl.when(jnp.logical_and(zp < early, zp + i < nc))
         def _():
@@ -110,7 +127,7 @@
     loads[3].wait()
     to_rows(jnp.max(jnp.abs(acol[...].astype(jnp.float32)), axis=0, keepdims=True), 16, nc)
 
-    pl.semaphore_wait(bar, 6 + jnp.minimum(zp, early))
+    pl.semaphore_wait(bar, 10 + jnp.minimum(zp, early))
     for i in range(early):
         @pl.when(i < zp)
         def _():
@@ -177,15 +194,14 @@
     def kind_a(s):
         if isinstance(s, int) and s == nc:
             return True
-        return s % 7 == 0
+        return s % 1 == 0
 
     def kind_c(s):
         if isinstance(s, int) and s == nc:
             return False
-        return s % 7 != 0
+        return s % 1 != 0
 
     def stage_own(s):
-        y_copy(s).start()
         xo_copy(s, 0).start()
         xo_copy(s, 1).start()
 
@@ -242,18 +258,31 @@
         cond(kind_a(s), kind_a_work)
         cond(kind_c(s), kind_c_work)
 
+    y_copy(nc).start()
     stage_own(nc)
     for s in range(nc):
         load_g(s).wait()
-        if s < 3:
+        if s < min(4, AHEAD + 1):
+            y_copy(s).start()
+        if s < min(3, AHEAD):
             stage_own(s)
+
+    def p2_copy():
+        return rcopy(pv, pcore, sp2, rp2, other_core)
 
     loads[2].wait()
     gscale = QUANT_LIMIT / jnp.maximum(jnp.max(gh[...], axis=0, keepdims=True), SCALE_FLOOR)
-    gscale_out[...] = gscale
     pad = jnp.zeros((1, wp - width), jnp.float32)
     gcol[...] = jnp.broadcast_to(jnp.concatenate([gscale, pad], axis=1), (LANES, wp)).T
     loads[4].wait()
+    loads[5].wait()
+    for i in range(nt):
+        at = nc * LANES + i * width
+
+        @pl.when(t == i)
+        def _():
+            gsl[...] = sl[:, at : at + width]
+
 
     def quant_rows(at, count):
         scale = gcol[at, :]
@@ -271,18 +300,23 @@
         return carry
 
     full = width // BLOCK
-    lax.fori_loop(0, full // 3, quant_block, 0)
-    stage_partner(nc)
-    stage_partner(0)
-    stage_far_own(nc)
-    stage_far_own(0)
-    lax.fori_loop(full // 3, 2 * full // 3, quant_block, 0)
-    if nc > 1:
-        stage_partner(1)
-        stage_far_own(1)
-    stage_far_other(nc)
-    stage_far_other(0)
-    lax.fori_loop(2 * full // 3, full, quant_block, 0)
+    for j in range(1, AHEAD):
+        if j <= 3:
+            lax.fori_loop((j - 1) * full // 3, j * full // 3, quant_block, 0)
+        if j == 1:
+            stage_partner(nc)
+            stage_far_own(nc)
+        if j == 2:
+            stage_far_other(nc)
+        if j - 1 < nc:
+            stage_partner(j - 1)
+            stage_far_own(j - 1)
+        if 0 <= j - 2 < min(AHEAD - 3, nc):
+            stage_far_other(j - 2)
+        if j + 3 < min(AHEAD + 1, nc):
+            y_copy(j + 3).start()
+        if j + 2 < min(AHEAD, nc):
+            stage_own(j + 2)
     if width > full * BLOCK:
         quant_rows(slice(full * BLOCK, width), width - full * BLOCK)
     gq[width:, :] = jnp.zeros((wp - width, tokens), jnp.bfloat16)
@@ -298,22 +332,16 @@
     ascale = QUANT_LIMIT / jnp.maximum(total_small[0:8, :], SCALE_FLOOR)
     for k in range(nc):
         scales[k] = ascale[k : k + 1, :]
-        ascale_out[:, k * LANES : (k + 1) * LANES] = ascale[k : k + 1, :]
     hb[...] = total_small[8:16, :]
     ch[pl.ds(hrow, 8), pl.ds(hcol, LANES)] = total_small[8:16, :]
     pv[0:8, :] = apeak
     for k in range(wp // LANES):
         pv[8 + k : 9 + k, :] = gpeak[:, k * LANES : (k + 1) * LANES]
     pv[8 + wp // LANES :, :] = jnp.zeros((8 - wp // LANES, LANES), jnp.float32)
+    p2_copy().start()
 
     def r1_copy(s):
         return rcopy(s1.at[s], r1.at[s], sr1.at[s], rr1.at[s], other_core)
-
-    def r2_copy(s):
-        return rcopy(s2.at[s], r2.at[s], sr2.at[s], rr2.at[s], other_yl)
-
-    def r3_copy(s):
-        return rcopy(s3.at[s], r3.at[s], sr3.at[s], rr3.at[s], other_z)
 
     def r4_copy(s):
         return rcopy(s4.at[s], rb.at[zp], sr4.at[s], rr4.at[zp], pair_dev(chunk(s)))
@@ -325,37 +353,68 @@
             q[pl.ds(i * rows, rows), :] = jnp.clip(v, -QUANT_LIMIT, QUANT_LIMIT).astype(jnp.bfloat16)
         out = jnp.dot(gq[...], q[...], preferred_element_type=jnp.float32)
         part[...] = out.T.reshape(8, 16, wp)
+
+    def start_r1(s):
         for i in range(4):
             s1[s, i] = part[2 * i + 1 - c].astype(jnp.bfloat16)
+        r1_copy(s).start()
+
+    def direct_copy(s, i):
+        zz, yy, cc = cube_index(i)
+        k = s - chain
+        return rcopy(
+            sd.at[k, zz * 4 + yy * 2 + cc], rd.at[k, i], srd.at[k, i], rrd.at[k, i], cube_dev(i)
+        )
+
+    def start_direct(s):
+        sd[s - chain] = part[...].astype(jnp.bfloat16)
+        keepd[s - chain] = part[zq * 4 + yl * 2 + c]
+        for i in range(1, 8):
+            direct_copy(s, i).start()
+
+    def finish_direct(s):
+        total = keepd[s - chain]
+        for i in range(1, 8):
+            direct_copy(s, i).wait_recv()
+            total = total + rd[s - chain, i].astype(jnp.float32)
+        emit(s, total)
+
+    def quad_copy(s, i):
+        zz, yy, _ = cube_index(2 * i)
+        return rcopy(
+            s2.at[s, i], r2.at[s, i], sr2.at[s, i], rr2.at[s, i], dp_dev(2 * zp + zz, yy, c)
+        )
 
     def finish_r1(s):
         r1_copy(s).wait_recv()
-        for zo in range(2):
-            a = 2 * zo + 1 - yl
-            b = 2 * zo + yl
-            s2[s, zo] = (part[2 * a + c] + r1[s, a].astype(jnp.float32)).astype(jnp.bfloat16)
-            keep2[zo] = part[2 * b + c] + r1[s, b].astype(jnp.float32)
-        r2_copy(s).start()
-
-    def finish_r2(s):
-        r2_copy(s).wait_recv()
-        s3[s] = (keep2[1 - zq] + r2[s, 1 - zq].astype(jnp.float32)).astype(jnp.bfloat16)
-        keep3[s] = keep2[zq] + r2[s, zq].astype(jnp.float32)
-        r3_copy(s).start()
-
-    def finish_r3(s):
-        r3_copy(s).wait_recv()
-        total = keep3[s] + r3[s].astype(jnp.float32)
+        for i in range(4):
+            zz, yy, _ = cube_index(2 * i)
+            k = 2 * zz + yy
+            total = part[2 * k + c] + r1[s, k].astype(jnp.float32)
+            if i == 0:
+                keep2[s % 2] = total
+            else:
+                s2[s, i] = total.astype(jnp.bfloat16)
+        for i in range(1, 4):
+            quad_copy(s, i).start()
+
+    def finish_quad(s):
+        total = keep2[s % 2]
+        for i in range(1, 4):
+            quad_copy(s, i).wait_recv()
+            total = total + r2[s, i].astype(jnp.float32)
+        emit(s, total)
+
+    def emit(s, total):
         s4[s] = total.astype(jnp.bfloat16)
-        own_sum[...] = total
-
-    def start_r4(s):
+
+        @pl.when(chunk(s) == zp)
+        def _():
+            own_sum[...] = total
+
         @pl.when(chunk(s) != zp)
         def _():
             r4_copy(s).start()
-
-    def p2_copy():
-        return rcopy(pv, pcore, sp2, rp2, other_core)
 
     def p3_copy():
         return rcopy(pcore, pylo, sp3, rp3, other_yl)
@@ -402,12 +461,7 @@
             for i in range(1, nc):
                 p5_copy(i).start()
 
-        def h4():
-            for i in range(1, nc):
-                h3_arrival(i).wait_recv()
-            h4_copy().start()
-
-        todo = [(0, p2_copy().start), (1, p3), (2, p4), (tok_step + 1, far), (6, h4)]
+        todo = [(0, p3), (1, p4), (2, far)]
         for at, work in todo:
             pl.when(s == min(at, nc - 1))(work)
 
@@ -425,74 +479,91 @@
             pl.semaphore_wait(tok2, 1)
 
     def step(s, carry):
-        @pl.when(s + 3 < nc)
-        def _():
-            stage_own(s + 3)
-
-        @pl.when(s >= 1)
+        @pl.when(s + AHEAD + 1 < nc)
+        def _():
+            y_copy(s + AHEAD + 1).start()
+
+        @pl.when(s + AHEAD < nc)
+        def _():
+            stage_own(s + AHEAD)
+
+        @pl.when(jnp.logical_and(s >= 1, s - 1 < chain))
         def _():
             finish_r1(s - 1)
-
-        @pl.when(s + 2 < nc)
-        def _():
-            stage_partner(s + 2)
-            stage_far_own(s + 2)
-
-        @pl.when(s + 1 < nc)
-        def _():
-            stage_far_other(s + 1)
-
-        @pl.when(s >= 2)
-        def _():
-            finish_r3(s - 2)
-
-        @pl.when(s == tok_step)
-        def _():
-            tokens_wait()
-            for i in range(max(tok_step - 2, 0)):
-                start_r4(i)
-
-        @pl.when(jnp.logical_and(s >= tok_step, s >= 2))
-        def _():
-            start_r4(s - 2)
 
         stage_finish(s)
         compute(s)
-        r1_copy(s).start()
-
-        @pl.when(s >= 1)
-        def _():
-            finish_r2(s - 1)
+
+        @pl.when(s < chain)
+        def _():
+            start_r1(s)
+
+        @pl.when(s >= chain)
+        def _():
+            start_direct(s)
+
+        @pl.when(jnp.logical_and(s == 0, AHEAD - 3 < nc))
+        def _():
+            stage_far_other(s + AHEAD - 3)
+
+        @pl.when(s + AHEAD - 1 < nc)
+        def _():
+            stage_partner(s + AHEAD - 1)
+            stage_far_own(s + AHEAD - 1)
+
+        @pl.when(s == tok_step)
+        def _():
+            tokens_wait()
+
+        @pl.when(jnp.logical_and(s >= 2, s - 2 < chain))
+        def _():
+            finish_quad(s - 2)
+
+        @pl.when(s + AHEAD - 2 < nc)
+        def _():
+            stage_far_other(s + AHEAD - 2)
+
+        @pl.when(s >= chain + 1)
+        def _():
+            finish_direct(s - 1)
 
         side_work(s)
         return carry
 
     lax.fori_loop(0, nc, step, 0)
     last = nc - 1
-    finish_r1(last)
-    if nc > 1:
-        finish_r3(last - 1)
-        start_r4(last - 1)
-    h4_arrival().wait_recv()
-    hist_out[...] = ch[...]
-    finish_r2(last)
+    for i in range(1, nc):
+        h3_arrival(i).wait_recv()
+    h4_copy().start()
+    if 0 <= last - 1 < chain:
+        finish_quad(last - 1)
     top = pzz[...]
     for i in range(1, nc):
         p5_copy(i).wait_recv()
         top = jnp.maximum(top, pfar[i])
     for k in range(nc):
-        peak_out[:, k * LANES : (k + 1) * LANES] = top[k : k + 1, :]
+        peak_row[:, k * LANES : (k + 1) * LANES] = top[k : k + 1, :]
     for k in range(wp // LANES):
         n = min(width - k * LANES, LANES)
-        gpeak_out[:, k * LANES : k * LANES + n] = top[8 + k : 9 + k, :n]
-    finish_r3(last)
+        gpeak_row[:, k * LANES : k * LANES + n] = top[8 + k : 9 + k, :n]
+    hist_row = lax.broadcasted_iota(jnp.int32, ghist_out.shape, 0)
+    ghist_out[...] = jnp.where(hist_row == gsl[...], gpeak_row[...], gh[...])
+    h4_arrival().wait_recv()
+    hist_row = lax.broadcasted_iota(jnp.int32, hist_out.shape, 0)
+    hist_out[...] = jnp.where(hist_row == sl[:, : nc * LANES], peak_row[...], ch[...])
+    lane = lax.broadcasted_iota(jnp.int32, (16, LANES), 1)
+    row = lax.broadcasted_iota(jnp.int32, (16, LANES), 0)
+    mine = lane == row + (zq * 4 + yl * 2 + c) * 16
+    row_scale = jnp.sum(jnp.where(mine, scales[zp], jnp.float32(0.0)), axis=1, keepdims=True)
+    gscale = QUANT_LIMIT / jnp.maximum(jnp.max(gh[...], axis=0, keepdims=True), SCALE_FLOOR)
+    finish_direct(last)
 
     total = own_sum[...]
     for i in range(1, nc):
         frm = (zp + i) % nc
         rcopy(rb.at[frm], rb.at[frm], sr4.at[0], rr4.at[frm], other_core).wait_recv()
         total = total + rb[frm].astype(jnp.float32)
-    sum_out[...] = total[:, :width]
+    wgrad_out[...] = total[:, :width] / (row_scale * gscale) * factor
 
     def drain_gather(s):
         y_copy(s).wait_send()
@@ -505,9 +576,12 @@
 
     def drain(s, carry):
         drain_gather(s)
-        r1_copy(s).wait_send()
-        r2_copy(s).wait_send()
-        r3_copy(s).wait_send()
+
+        @pl.when(s < chain)
+        def _():
+            r1_copy(s).wait_send()
+            for i in range(1, 4):
+                quad_copy(s, i).wait_send()
 
         @pl.when(chunk(s) != zp)
         def _():
@@ -517,6 +591,9 @@
 
     drain_gather(nc)
     lax.fori_loop(0, nc, drain, 0)
+    for s in range(chain, nc):
+        for i in range(1, 8):
+            direct_copy(s, i).wait_send()
     h4_copy().wait_send()
     p2_copy().wait_send()
     p3_copy().wait_send()
@@ -526,7 +603,7 @@
         p5_copy(i).wait_send()
 
 
-def fused(acts, grads, ahist, ghist, owner, nz, nx):
+def fused(acts, grads, ahist, ghist, owner, slots, nz, nx, factor):
     rows, model = acts.shape
     width, tokens = grads.shape
     nc, nt = nz // 2, 2 * nx
@@ -543,6 +620,10 @@
         vm((1, 16, model), f32),
         vm((16, width), f32),
         vm((1, model), jnp.int32),
+        vm(slots.shape, jnp.int32),
+        vm((1, width), jnp.int32),
+        vm((1, model), f32),
+        vm((1, width), f32),
         vm((wp, LANES), f32),
         vm((wp, LANES), f32),
         vm((nc, 1, LANES), f32),
@@ -558,67 +639,50 @@
         vm((8, 16, wp), f32),
         vm((nc, 4, 16, wp), bf16),
         vm((nc, 4, 16, wp), bf16),
-        vm((nc, 2, 16, wp), bf16),
-        vm((nc, 2, 16, wp), bf16),
+        vm((nc, 4, 16, wp), bf16),
+        vm((nc, 4, 16, wp), bf16),
         vm((2, 16, wp), f32),
         vm((nc, 16, wp), bf16),
         vm((nc, 16, wp), bf16),
-        vm((nc, 16, wp), f32),
-        vm((nc, 16, wp), bf16),
-        vm((nc, 16, wp), bf16),
         vm((16, wp), f32),
-        dma((nc,)), dma((5,)),
+        vm((DIRECT, 8, 16, wp), bf16),
+        vm((DIRECT, 8, 16, wp), bf16),
+        vm((DIRECT, 16, wp), f32),
+        dma((nc,)), dma((6,)),
         dma((nc + 1,)), dma((nc + 1,)),
         dma((nc + 1, 2)), dma((nc + 1, 2)), dma((nc + 1, 2)), dma((nc + 1, 2)),
         dma((nc + 1, 2)), dma((nc + 1, 2)), dma((nc + 1,)), dma((nc + 1,)),
         dma((nc,)), dma((nc,)), dma, dma,
         dma, dma, dma, dma, dma, dma, dma((nc,)), dma((nc,)),
-        dma((nc,)), dma((nc,)), dma((nc,)), dma((nc,)),
-        dma((nc,)), dma((nc,)), dma((nc,)), dma((nc,)),
+        dma((nc,)), dma((nc,)), dma((nc, 4)), dma((nc, 4)), dma((nc,)), dma((nc,)),
+        dma((DIRECT, 8)), dma((DIRECT, 8)),
         pltpu.SemaphoreType.REGULAR, pltpu.SemaphoreType.REGULAR,
     ]
     vspec = pl.BlockSpec(memory_space=pltpu.VMEM)
     anyspec = pl.BlockSpec(memory_space=pl.ANY)
     return pl.pallas_call(
-        functools.partial(kernel, nz, nx),
+        functools.partial(kernel, nz, nx, factor),
         out_shape=[
             jax.ShapeDtypeStruct((16, width), f32),
             jax.ShapeDtypeStruct((16, model), f32),
-            jax.ShapeDtypeStruct((1, model), f32),
-            jax.ShapeDtypeStruct((1, width), f32),
-            jax.ShapeDtypeStruct((1, model), f32),
-            jax.ShapeDtypeStruct((1, width), f32),
+            jax.ShapeDtypeStruct((16, width), f32),
         ],
-        in_specs=[anyspec] * 5,
-        out_specs=[vspec] * 6,
+        in_specs=[anyspec] * 6,
+        out_specs=[vspec] * 3,
         scratch_shapes=scratch,
         compiler_params=pltpu.CompilerParams(
-            collective_id=0, has_side_effects=True, vmem_limit_bytes=60 * 1024 * 1024
+            collective_id=0, has_side_effects=True, vmem_limit_bytes=54600 * 1024
         ),
-    )(acts, grads, ahist, ghist, owner)
+    )(acts, grads, ahist, ghist, owner, slots)
 
 
 def body(nz, nx, activations, gradients, act_history, grad_history, owner_rank, history_slot):
-    model = act_history.shape[2]
-    width = gradients.shape[1]
-    my_rank = lax.axis_index("tensor")
-    summed, current, act_peak, grad_peak, act_scale, grad_scale = fused(
-        activations, gradients.T, act_history, grad_history, owner_rank.reshape(1, model), nz, nx
+    factor = 1.0 / math.sqrt(gradients.shape[0] * lax.axis_size("dp"))
+    weight_grad, act_history_out, grad_history_out = fused(
+        activations, gradients.T, act_history, grad_history,
+        owner_rank.reshape(1, -1), history_slot.reshape(1, -1), nz, nx, factor,
     )
-    grad_factor = 1.0 / math.sqrt(gradients.shape[0] * lax.axis_size("dp"))
-    row_base = lax.axis_index("dp") * 16
-    row_scale = lax.dynamic_slice(act_scale, (0, row_base), (1, 16)).reshape(16, 1)
-    weight_grad = summed / (row_scale * grad_scale) * grad_factor
-    act_slots = history_slot[:model]
-    grad_slots = lax.dynamic_slice_in_dim(history_slot, model + my_rank * width, width, 0)
-
-    def place(history, peaks, slots):
-        at = lax.broadcasted_iota(jnp.int32, history.shape, 0)
-        return jnp.where(at == slots[None, :], peaks, history)
-
-    act_history_out = place(current, act_peak, act_slots)[None]
-    grad_history_out = place(grad_history, grad_peak, grad_slots)
-    return (weight_grad, act_history_out, grad_history_out)
+    return (weight_grad, act_history_out[None], grad_history_out)
 
 
 def solution(mesh):

time: 76.6 us -> 66.7 us (0.87)
  the two profiles are of different devices: /device:TPU:4 before, /device:TPU:384 now
where the time goes in v3:
time: 66.7 us; the launch traced here: 66.4 us
  Pallas kernels  60.8 us (91%)
  local copies, waits for them, and re-layouts  4.96 us (7%)
    pallas_call x1, Pallas kernels, fused(): pl.pallas_call(functools.partial(kernel, nz, nx, factor), out_shape=[jax....  60.8 us
    unnamed x9, local copies, waits for them, and re-layouts  4.19 us

profile of v3, /device:TPU:384, one launch (start us, length us, event | category | flops | bytes accessed | tf_op | source)
XLA Modules:
  0.0 66.4 jit_solution(521777067145778198)
XLA Ops:
  0.6 0.8 %reshape.13.slots = s32[1,6496]{1,0:T(1,128)S(1)} reshape(s32[6496]{0:T(1024)} %param.11) | data formatting | bytes 51968 | tf_op jit(solution)/shard_map/reshape | solution.py:683
  1.4 0.0 copy-start
  1.4 0.8 %copy-done = f32[1,16,1024]{2,1,0:T(8,128)S(1)} copy-done((f32[1,16,1024]{2,1,0:T(8,128)S(1)}, f32[1,16,1024]{2,1,0:T(8,128)}, u32[]{:S(2)}) %copy-start) | copy-done | bytes 65560
  2.2 0.0 copy-start.1
  2.2 0.8 %copy-done.1 = f32[16,684]{1,0:T(8,128)S(1)} copy-done((f32[16,684]{1,0:T(8,128)S(1)}, f32[16,684]{1,0:T(8,128)}, u32[]{:S(2)}) %copy-start.1) | copy-done | bytes 43800
  3.0 0.0 copy-start.2
  3.0 0.7 %copy-done.2 = s32[1024]{0:T(1024)S(1)} copy-done((s32[1024]{0:T(1024)S(1)}, s32[1024]{0:T(1024)}, u32[]{:S(2)}) %copy-start.2) | copy-done | bytes 4120
  3.7 60.8 %shard_map.85 = (f32[16,684]{1,0:T(8,128)S(1)}, f32[16,1024]{1,0:T(8,128)S(1)}, f32[16,684]{1,0:T(8,128)S(1)}) custom-call(bf16[256,1024]{1,0:T(8,128)(2,1)} %acts.1, bf16[684,2048]{1,0:T(8,128)(2,1)} %bitcast.5, f32[1,16,1024]{2,1,0:T(8,128)S(1)} %copy-done, f32[16,684]{1,0:T(8,128)S(1)} %copy-done.1, s32[1,1024]{1,0:T(1,128)S(1)} %bitcast.4, ...), custom_call_target="tpu_custom_call" | custom-call | tf_op jit(solution)/shard_map/pallas_call | solution.py:663
  64.5 0.6 copy.12
  65.1 0.6 copy.13
  65.7 0.6 copy.14
Async XLA Ops:
  1.4 0.8 %copy-start = (f32[1,16,1024]{2,1,0:T(8,128)S(1)}, f32[1,16,1024]{2,1,0:T(8,128)}, u32[]{:S(2)}) copy-start(f32[1,16,1024]{2,1,0:T(8,128)} %ahist.1) | copy-start | bytes 196612
  2.2 0.8 %copy-start.1 = (f32[16,684]{1,0:T(8,128)S(1)}, f32[16,684]{1,0:T(8,128)}, u32[]{:S(2)}) copy-start(f32[16,684]{1,0:T(8,128)} %ghist.1) | copy-start | bytes 131332
  3.0 0.7 %copy-start.2 = (s32[1024]{0:T(1024)S(1)}, s32[1024]{0:T(1024)}, u32[]{:S(2)}) copy-start(s32[1024]{0:T(1024)} %param.10) | copy-start | bytes 12292

commit v4 on v3

v4 whole, which is shorter than its diff:
```python
import functools
import math

import jax
import jax.numpy as jnp
from jax import lax
from jax.experimental import pallas as pl
from jax.experimental.pallas import tpu as pltpu
from jax.sharding import PartitionSpec as P

QUANT_LIMIT = 448.0
SCALE_FLOOR = 0.25
LANES = 128
BLOCK = 64
AHEAD = 4
MESH = pl.DeviceIdType.MESH


def kernel(
    nz, nx, factor, acts, grads, ahist, ghist, owner, slots,
    wgrad_out, hist_out, ghist_out,
    g, acol, graw, gq, q, ah, gh, ow, sl, gsl, peak_row, gpeak_row, gcol, gpk, scales, mh, small, hb, ch,
    pv, pcore, pylo, pzz, pfar,
    part, s1, r1, s2, r2, keep2, s4, rb, own_sum,
    ld_g, ld_x,
    sg, rg,
    sh3, rh3, sh4, rh4, sp2, rp2, sp3, rp3, sp4, rp4, sp5, rp5,
    sr1, rr1, sr2, rr2, sr4, rr4, tok1, tok2,
):
    nc = nz // 2
    nt = 2 * nx
    early = max(3 * nc // 8, 1)
    tok_step = min(1, nc - 1)
    rows = acts.shape[0]
    width, tokens = grads.shape
    wp = gq.shape[0]
    t = lax.axis_index("tensor")
    dpi = lax.axis_index("dp")
    x, yh = t // 2, t % 2
    z, yl, c = dpi // 4, (dpi // 2) % 2, dpi % 2
    zp, zq = z // 2, z % 2
    xr, xl, xf = (x + 1) % nx, (x + nx - 1) % nx, (x + 2) % nx
    yo = 1 - yh

    def tensor_dev(tt):
        return {"dp": dpi, "tensor": tt}

    def dp_dev(zz, yy, cc):
        return {"dp": zz * 4 + yy * 2 + cc, "tensor": t}

    def pair_dev(pp):
        return dp_dev(2 * pp + zq, yl, c)

    def rcopy(src, dst, ss, rs, device):
        return pltpu.make_async_remote_copy(
            src_ref=src, dst_ref=dst, send_sem=ss, recv_sem=rs,
            device_id=device, device_id_type=MESH,
        )

    def signal(sem, device):
        pl.semaphore_signal(sem, inc=1, device_id=device, device_id_type=MESH)

    def chunk(s):
        hf = nc // 2
        late = s // hf
        j = 2 * hf - 1 - s
        high = zp // hf
        u = high * (zp - hf) + (1 - high) * (hf - 1 - zp)
        flip = (u + j) % 2 + 2 * ((u // 2 + j // 2) % 2)
        return (1 - late) * s + late * (hf + flip % hf)

    partner_y = tensor_dev(2 * x + yo)
    right = tensor_dev(2 * xr + yh)
    left = tensor_dev(2 * xl + yh)
    other_core = dp_dev(z, yl, 1 - c)
    other_yl = dp_dev(z, 1 - yl, c)
    other_z = dp_dev(2 * zp + 1 - zq, yl, c)

    def cube_index(i):
        return (zq + i // 4) % 2, (yl + i // 2 % 2) % 2, (c + i % 2) % 2

    def cube_dev(i):
        zz, yy, cc = cube_index(i)
        return dp_dev(2 * zp + zz, yy, cc)

    def load_g(s):
        col = pl.multiple_of(chunk(s) * LANES, LANES)
        return pltpu.make_async_copy(
            acts.at[:, pl.ds(col, LANES)], g.at[s * nt + t], ld_g.at[min(s, 1)]
        )

    loads = [
        pltpu.make_async_copy(src, dst, ld_x.at[i])
        for i, (src, dst) in enumerate(
            [(ahist, ah), (owner, ow), (ghist, gh), (acts, acol), (grads, graw), (slots, sl.at[0])]
        )
    ]
    bar = pltpu.get_barrier_semaphore()
    for device in (partner_y, right, left):
        signal(bar, device)
    for i in range(1, 8):
        signal(bar, cube_dev(i))
    for i in range(1, nc):
        @pl.when(jnp.logical_and(zp < early, zp + i < nc))
        def _():
            signal(bar, pair_dev(zp + i))

    load_g(0).start()
    for i in (0, 1, 3):
        loads[i].start()
    for s in range(1, nc):
        load_g(s).start()
    for i in (2, 4, 5):
        loads[i].start()

    def to_rows(vec, at, count):
        for k in range(count):
            small[t, at + k : at + k + 1, :] = vec[:, k * LANES : (k + 1) * LANES]

    pl.semaphore_wait(bar, 10 + jnp.minimum(zp, early))
    for i in range(early):
        @pl.when(i < zp)
        def _():
            signal(tok1, pair_dev(i))

    def at_slot(s, xx, yy):
        if isinstance(s, int) and s == nc:
            return small.at[2 * xx + yy]
        return g.at[s * nt + 2 * xx + yy]

    def slots_of(s, count):
        return (small if isinstance(s, int) and s == nc else g).at[pl.ds(0, count)]

    def send(s, a, k, device):
        done = sg.at[1 if isinstance(s, int) and s == nc else 0]
        rcopy(a, a, done, rg.at[s, k], device).start()

    def arrived(s, k, count=1):
        a = slots_of(s, count)
        rcopy(a, a, sg.at[0], rg.at[s, k], partner_y).wait_recv()

    def cond(pred, work):
        if isinstance(pred, bool):
            if pred:
                work()
        else:
            pl.when(pred)(work)

    def start_y(s):
        send(s, at_slot(s, x, yh), 0, partner_y)

    def stage_own(s):
        a = at_slot(s, x, yh)
        send(s, a, 1 + 2 * (s % 2), right)
        send(s, a, 1 + 2 * ((s + 1) % 2), left)

    def stage_partner(s):
        arrived(s, 0)
        a = at_slot(s, x, yo)
        send(s, a, 3 - s % 2, right)
        send(s, a, 3 - (s + 1) % 2, left)

    def stage_far_own(s):
        arrived(s, 1)
        cond(s % 2 == 0, lambda: send(s, at_slot(s, xl, yh), 3, right))
        cond(s % 2 == 1, lambda: send(s, at_slot(s, xr, yh), 3, left))

    def stage_far_other(s):
        arrived(s, 2)
        cond(s % 2 == 0, lambda: send(s, at_slot(s, xr, yo), 3, left))
        cond(s % 2 == 1, lambda: send(s, at_slot(s, xl, yo), 3, right))

    def stage_finish(s):
        arrived(s, 3, 4)

    load_g(0).wait()
    start_y(0)
    stage_own(0)
    loads[0].wait()
    loads[1].wait()
    held = jnp.where(ow[...] == t, ah[0], jnp.float32(0.0))
    mh[...] = held
    to_rows(jnp.max(held, axis=0, keepdims=True), 0, nc)
    hcol = pl.multiple_of(zp * LANES, LANES)
    hrow = pl.multiple_of(c * 8, 8)
    small[t, 8:16, :] = mh[pl.ds(hrow, 8), pl.ds(hcol, LANES)]
    loads[3].wait()
    to_rows(jnp.max(jnp.abs(acol[...].astype(jnp.float32)), axis=0, keepdims=True), 16, nc)

    start_y(nc)
    stage_own(nc)
    rest = acol.at[:, pl.ds(0, (nc - 1) * LANES)]
    pltpu.make_async_copy(rest, rest, ld_g.at[1]).wait()
    for s in range(1, min(4, nc)):
        start_y(s)
        if s < min(3, AHEAD):
            stage_own(s)

    def p2_copy():
        return rcopy(pv, pcore, sp2, rp2, other_core)

    loads[2].wait()
    gscale = QUANT_LIMIT / jnp.maximum(jnp.max(gh[...], axis=0, keepdims=True), SCALE_FLOOR)
    pad = jnp.zeros((1, wp - width), jnp.float32)
    gcol[...] = jnp.broadcast_to(jnp.concatenate([gscale, pad], axis=1), (LANES, wp)).T
    loads[4].wait()
    loads[5].wait()
    for i in range(nt):
        at = nc * LANES + i * width

        @pl.when(t == i)
        def _():
            gsl[...] = sl[:, at : at + width]


    def quant_rows(at, count):
        scale = gcol[at, :]
        top = jnp.zeros((count, LANES), jnp.float32)
        for j in range(tokens // LANES):
            v = graw[at, j * LANES : (j + 1) * LANES].astype(jnp.float32)
            gq[at, j * LANES : (j + 1) * LANES] = jnp.clip(
                v * scale, -QUANT_LIMIT, QUANT_LIMIT
            ).astype(jnp.bfloat16)
            top = jnp.maximum(top, jnp.abs(v))
        gpk[at, :] = top

    def quant_block(i, carry):
        quant_rows(pl.ds(pl.multiple_of(i * BLOCK, BLOCK), BLOCK), BLOCK)
        return carry

    full = width // BLOCK
    for j in range(1, AHEAD):
        if j <= 3:
            lax.fori_loop((j - 1) * full // 3, j * full // 3, quant_block, 0)
        if j - 1 < nc:
            stage_partner(j - 1)
            stage_far_own(j - 1)
        if j == 1:
            stage_partner(nc)
            stage_far_own(nc)
        if j == 2:
            stage_far_other(nc)
        if 0 <= j - 2 < min(AHEAD - 3, nc):
            stage_far_other(j - 2)
        if j + 3 < min(AHEAD + 1, nc):
            start_y(j + 3)
        if j + 2 < min(AHEAD, nc):
            stage_own(j + 2)
    if width > full * BLOCK:
        quant_rows(slice(full * BLOCK, width), width - full * BLOCK)
    gq[width:, :] = jnp.zeros((wp - width, tokens), jnp.bfloat16)
    gpk[width:, :] = jnp.zeros((wp - width, LANES), jnp.float32)
    gpeak = jnp.max(gpk[...].T, axis=0, keepdims=True)

    stage_finish(nc)
    total_small = small[0]
    apeak = small[0, 16:24, :]
    for i in range(1, nt):
        total_small = total_small + small[i]
        apeak = jnp.maximum(apeak, small[i, 16:24, :])
    ascale = QUANT_LIMIT / jnp.maximum(total_small[0:8, :], SCALE_FLOOR)
    for k in range(nc):
        scales[k] = ascale[k : k + 1, :]
    hb[...] = total_small[8:16, :]
    ch[pl.ds(hrow, 8), pl.ds(hcol, LANES)] = total_small[8:16, :]
    pv[0:8, :] = apeak
    for k in range(wp // LANES):
        pv[8 + k : 9 + k, :] = gpeak[:, k * LANES : (k + 1) * LANES]
    pv[8 + wp // LANES :, :] = jnp.zeros((8 - wp // LANES, LANES), jnp.float32)
    p2_copy().start()

    def r1_copy(s):
        return rcopy(s1.at[s], r1.at[s], sr1, rr1.at[s], other_core)

    def r4_copy(s):
        return rcopy(s4.at[s], rb.at[zp], sr4, rr4, pair_dev(chunk(s)))

    def compute(s):
        scale = scales[chunk(s)]
        for i in range(nt):
            v = g[s * nt + i].astype(jnp.float32) * scale
            q[pl.ds(i * rows, rows), :] = jnp.clip(v, -QUANT_LIMIT, QUANT_LIMIT).astype(jnp.bfloat16)
        out = jnp.dot(gq[...], q[...], preferred_element_type=jnp.float32)
        part[...] = out.T.reshape(8, 16, wp)

    def start_r1(s):
        for i in range(4):
            s1[s, i] = part[2 * i + 1 - c].astype(jnp.bfloat16)
        r1_copy(s).start()

    def quad_copy(s, i):
        zz, yy, _ = cube_index(2 * i)
        return rcopy(
            s2.at[s * 3 + i - 1], r2.at[s * 3 + i - 1], sr2, rr2.at[s], dp_dev(2 * zp + zz, yy, c)
        )

    def finish_r1(s):
        r1_copy(s).wait_recv()
        for i in range(4):
            zz, yy, _ = cube_index(2 * i)
            k = 2 * zz + yy
            total = part[2 * k + c] + r1[s, k].astype(jnp.float32)
            if i == 0:
                keep2[s % 4] = total
            else:
                s2[s * 3 + i - 1] = total.astype(jnp.bfloat16)
        for i in range(1, 4):
            quad_copy(s, i).start()

    def finish_quad(s):
        total = keep2[s % 4]
        a = r2.at[pl.ds(s * 3, 3)]
        rcopy(a, a, sr2, rr2.at[s], other_core).wait_recv()
        for i in range(3):
            total = total + r2[s * 3 + i].astype(jnp.float32)
        emit(s, total)

    def emit(s, total):
        s4[s] = total.astype(jnp.bfloat16)

        @pl.when(chunk(s) == zp)
        def _():
            own_sum[...] = total

        @pl.when(chunk(s) != zp)
        def _():
            r4_copy(s).start()

    def p3_copy():
        return rcopy(pcore, pylo, sp3, rp3, other_yl)

    def p4_copy():
        return rcopy(pylo, pzz, sp4, rp4, other_z)

    def p5_copy(i):
        return rcopy(pzz, pfar.at[i], sp5, rp5, pair_dev((zp + i) % nc))

    def h3_copy(i):
        dst = ch.at[pl.ds(hrow, 8), pl.ds(hcol, LANES)]
        return rcopy(hb, dst, sh3, rh3, pair_dev((zp + i) % nc))

    def h3_all():
        a = ch.at[pl.ds(0, 8), pl.ds(0, (nc - 1) * LANES)]
        return rcopy(a, a, sh3, rh3, other_core)

    def p5_all():
        a = pfar.at[pl.ds(1, nc - 1)]
        return rcopy(a, a, sp5, rp5, other_core)

    def h4_copy():
        half = ch.at[pl.ds(hrow, 8), :]
        return rcopy(half, half, sh4, rh4, other_core)

    def h4_arrival():
        half = ch.at[pl.ds(pl.multiple_of(8 - hrow, 8), 8), :]
        return rcopy(half, half, sh4, rh4, other_core)

    def side_work(s):
        def p3():
            p2_copy().wait_recv()
            pcore[...] = jnp.maximum(pcore[...], pv[...])
            p3_copy().start()

        def p4():
            p3_copy().wait_recv()
            pylo[...] = jnp.maximum(pylo[...], pcore[...])
            p4_copy().start()

        def far():
            p4_copy().wait_recv()
            pzz[...] = jnp.maximum(pzz[...], pylo[...])
            for i in range(1, nc):
                h3_copy(i).start()
            for i in range(1, nc):
                p5_copy(i).start()

        todo = [(0, p3), (1, p4), (2, far)]
        for at, work in todo:
            pl.when(s == min(at, nc - 1))(work)

    def tokens_wait():
        @pl.when(zp < early)
        def _():
            pl.semaphore_wait(tok1, nc - 1 - zp)
            for pp in range(early, nc):
                @pl.when((nc - 1 - pp) % early == zp)
                def _():
                    signal(tok2, pair_dev(pp))

        @pl.when(zp >= early)
        def _():
            pl.semaphore_wait(tok2, 1)

    def step(s, carry):
        @pl.when(s + AHEAD + 1 < nc)
        def _():
            start_y(s + AHEAD + 1)

        @pl.when(s + AHEAD < nc)
        def _():
            stage_own(s + AHEAD)

        @pl.when(s >= 1)
        def _():
            finish_r1(s - 1)

        stage_finish(s)
        compute(s)
        start_r1(s)

        @pl.when(jnp.logical_and(s == 0, AHEAD - 3 < nc))
        def _():
            stage_far_other(s + AHEAD - 3)

        @pl.when(s + AHEAD - 1 < nc)
        def _():
            stage_partner(s + AHEAD - 1)
            stage_far_own(s + AHEAD - 1)

        @pl.when(s == tok_step)
        def _():
            tokens_wait()

        @pl.when(jnp.logical_and(s >= 2, s < nc - 1))
        def _():
            finish_quad(s - 2)

        @pl.when(s + AHEAD - 2 < nc)
        def _():
            stage_far_other(s + AHEAD - 2)

        side_work(s)
        return carry

    lax.fori_loop(0, nc, step, 0)
    last = nc - 1
    finish_r1(last)
    if nc > 2:
        finish_quad(last - 2)
    h3_all().wait_recv()
    h4_copy().start()
    if nc > 1:
        finish_quad(last - 1)
    top = pzz[...]
    p5_all().wait_recv()
    for i in range(1, nc):
        top = jnp.maximum(top, pfar[i])
    for k in range(nc):
        peak_row[:, k * LANES : (k + 1) * LANES] = top[k : k + 1, :]
    for k in range(wp // LANES):
        n = min(width - k * LANES, LANES)
        gpeak_row[:, k * LANES : k * LANES + n] = top[8 + k : 9 + k, :n]
    hist_row = lax.broadcasted_iota(jnp.int32, ghist_out.shape, 0)
    ghist_out[...] = jnp.where(hist_row == gsl[...], gpeak_row[...], gh[...])
    h4_arrival().wait_recv()
    hist_row = lax.broadcasted_iota(jnp.int32, hist_out.shape, 0)
    hist_out[...] = jnp.where(hist_row == sl[:, : nc * LANES], peak_row[...], ch[...])
    lane = lax.broadcasted_iota(jnp.int32, (16, LANES), 1)
    row = lax.broadcasted_iota(jnp.int32, (16, LANES), 0)
    mine = lane == row + (zq * 4 + yl * 2 + c) * 16
    row_scale = jnp.sum(jnp.where(mine, scales[zp], jnp.float32(0.0)), axis=1, keepdims=True)
    gscale = QUANT_LIMIT / jnp.maximum(jnp.max(gh[...], axis=0, keepdims=True), SCALE_FLOOR)
    finish_quad(last)

    total = own_sum[...]
    a = rb.at[pl.ds(0, nc - 1)]
    rcopy(a, a, sr4, rr4, other_core).wait_recv()
    for i in range(1, nc):
        frm = (zp + i) % nc
        total = total + rb[frm].astype(jnp.float32)
    wgrad_out[...] = total[:, :width] / (row_scale * gscale) * factor

    for a, done in (
        (g.at[pl.ds(0, 7 * nc)], sg.at[0]),
        (small.at[pl.ds(0, 7)], sg.at[1]),
        (s1, sr1),
        (s2, sr2),
        (s4.at[pl.ds(0, nc - 1)], sr4),
    ):
        rcopy(a, a, done, rr4, other_core).wait_send()
    h4_copy().wait_send()
    p2_copy().wait_send()
    p3_copy().wait_send()
    p4_copy().wait_send()
    h3_all().wait_send()
    p5_all().wait_send()


def fused(acts, grads, ahist, ghist, owner, slots, nz, nx, factor):
    rows, model = acts.shape
    width, tokens = grads.shape
    nc, nt = nz // 2, 2 * nx
    wp = -(-width // LANES) * LANES
    f32, bf16 = jnp.float32, jnp.bfloat16
    dma = pltpu.SemaphoreType.DMA
    vm = pltpu.VMEM
    scratch = [
        vm((nc * nt, rows, LANES), bf16),
        vm((rows, model), bf16),
        vm((width, tokens), bf16),
        vm((wp, tokens), bf16),
        vm((tokens, LANES), bf16),
        vm((1, 16, model), f32),
        vm((16, width), f32),
        vm((1, model), jnp.int32),
        vm((1, slots.shape[0]), jnp.int32),
        vm((1, width), jnp.int32),
        vm((1, model), f32),
        vm((1, width), f32),
        vm((wp, LANES), f32),
        vm((wp, LANES), f32),
        vm((nc, 1, LANES), f32),
        vm((16, model), f32),
        vm((nt, 24, LANES), f32),
        vm((8, LANES), f32),
        vm((16, model), f32),
        vm((16, LANES), f32),
        vm((16, LANES), f32),
        vm((16, LANES), f32),
        vm((16, LANES), f32),
        vm((nc, 16, LANES), f32),
        vm((8, 16, wp), f32),
        vm((nc, 4, 16, wp), bf16),
        vm((nc, 4, 16, wp), bf16),
        vm((nc * 3, 16, wp), bf16),
        vm((nc * 3, 16, wp), bf16),
        vm((4, 16, wp), f32),
        vm((nc, 16, wp), bf16),
        vm((nc, 16, wp), bf16),
        vm((16, wp), f32),
        dma((2,)), dma((6,)),
        dma((2,)), dma((nc + 1, 4)),
        dma, dma, dma, dma,
        dma, dma, dma, dma, dma, dma, dma, dma,
        dma, dma((nc,)), dma, dma((nc,)), dma, dma,
        pltpu.SemaphoreType.REGULAR, pltpu.SemaphoreType.REGULAR,
    ]
    vspec = pl.BlockSpec(memory_space=pltpu.VMEM)
    anyspec = pl.BlockSpec(memory_space=pl.ANY)
    return pl.pallas_call(
        functools.partial(kernel, nz, nx, factor),
        out_shape=[
            jax.ShapeDtypeStruct((16, width), f32),
            jax.ShapeDtypeStruct((16, model), f32),
            jax.ShapeDtypeStruct((16, width), f32),
        ],
        in_specs=[anyspec] * 6,
        out_specs=[vspec] * 3,
        scratch_shapes=scratch,
        compiler_params=pltpu.CompilerParams(
            collective_id=0, has_side_effects=True, vmem_limit_bytes=55100 * 1024
        ),
    )(acts, grads, ahist, ghist, owner, slots)


def body(nz, nx, activations, gradients, act_history, grad_history, owner_rank, history_slot):
    factor = 1.0 / math.sqrt(gradients.shape[0] * lax.axis_size("dp"))
    weight_grad, act_history_out, grad_history_out = fused(
        activations, gradients.T, act_history, grad_history,
        owner_rank.reshape(1, -1), history_slot, nz, nx, factor,
    )
    return (weight_grad, act_history_out[None], grad_history_out)


def solution(mesh):
    nz = mesh.shape["dp"] // 4
    nx = mesh.shape["tensor"] // 2
    placed = (
        P(("dp", "tensor"), None),
        P("dp", "tensor"),
        P("tensor", None, None),
        P(None, "tensor"),
        P(),
        P(),
    )
    return jax.shard_map(
        functools.partial(body, nz, nx),
        mesh=mesh,
        in_specs=placed,
        out_specs=(P("dp", "tensor"), P("tensor", None, None), P(None, "tensor")),
        check_vma=False,
    )
```

time: 66.7 us -> 64.4 us (0.966)
  the two profiles are of different devices: /device:TPU:384 before, /device:TPU:4 now
where the time goes in v4:
time: 64.4 us; the launch traced here: 64.1 us
  Pallas kernels  59.3 us (92%)
  local copies, waits for them, and re-layouts  4.14 us (6%)
  between operations  0.65 us (1%)
    pallas_call x1, Pallas kernels, fused(): pl.pallas_call(functools.partial(kernel, nz, nx, factor), out_shape=[jax....  59.3 us
    unnamed x7, local copies, waits for them, and re-layouts  4.14 us

profile of v4, /device:TPU:4, one launch (start us, length us, event | category | flops | bytes accessed | tf_op | source)
XLA Modules:
  0.0 64.1 jit_solution(4425914708224482031)
XLA Ops:
  0.6 0.0 copy-start
  0.6 0.7 %copy-done = s32[6496]{0:T(1024)S(1)} copy-done((s32[6496]{0:T(1024)S(1)}, s32[6496]{0:T(1024)}, u32[]{:S(2)}) %copy-start) | copy-done | bytes 26008
  1.4 0.0 copy-start.1
  1.4 0.7 %copy-done.1 = s32[1024]{0:T(1024)S(1)} copy-done((s32[1024]{0:T(1024)S(1)}, s32[1024]{0:T(1024)}, u32[]{:S(2)}) %copy-start.1) | copy-done | bytes 4120
  2.1 59.3 %shard_map.85 = (f32[16,684]{1,0:T(8,128)S(1)}, f32[16,1024]{1,0:T(8,128)}, f32[16,684]{1,0:T(8,128)S(1)}) custom-call(bf16[256,1024]{1,0:T(8,128)(2,1)} %acts.1, bf16[684,2048]{1,0:T(8,128)(2,1)} %bitcast.4, f32[1,16,1024]{2,1,0:T(8,128)} %ahist.1, f32[16,684]{1,0:T(8,128)} %ghist.1, s32[1,1024]{1,0:T(1,128)S(1)} %bitcast.3, s32[6496]{0:T(1024)S(1)} %copy-done), custom_call_target="tpu_custom_call" | custom-call | tf_op jit(solution)/shard_map/pallas_call | solution.py:540
  61.4 0.6 copy.12
  62.0 1.5 %copy.13 = f32[1,16,1024]{2,1,0:T(8,128)} copy(f32[1,16,1024]{2,1,0:T(8,128)} %bitcast.5) | data formatting | bytes 131072
  63.5 0.6 copy.14
Async XLA Ops:
  0.6 0.7 %copy-start = (s32[6496]{0:T(1024)S(1)}, s32[6496]{0:T(1024)}, u32[]{:S(2)}) copy-start(s32[6496]{0:T(1024)} %slots.1) | copy-start | bytes 77956
  1.4 0.7 %copy-start.1 = (s32[1024]{0:T(1024)S(1)}, s32[1024]{0:T(1024)}, u32[]{:S(2)}) copy-start(s32[1024]{0:T(1024)} %param.10) | copy-start | bytes 12292

commit v5 on v4

--- a/solution.py
+++ b/solution.py
@@ -17,8 +17,8 @@
 
 
 def kernel(
-    nz, nx, factor, acts, grads, ahist, ghist, owner, slots,
-    wgrad_out, hist_out, ghist_out,
+    nz, nx, acts, grads, ahist, ghist, owner, slots,
+    pack_out, hist_out,
     g, acol, graw, gq, q, ah, gh, ow, sl, gsl, peak_row, gpeak_row, gcol, gpk, scales, mh, small, hb, ch,
     pv, pcore, pylo, pzz, pfar,
     part, s1, r1, s2, r2, keep2, s4, rb, own_sum,
@@ -450,8 +450,8 @@
     for k in range(wp // LANES):
         n = min(width - k * LANES, LANES)
         gpeak_row[:, k * LANES : k * LANES + n] = top[8 + k : 9 + k, :n]
-    hist_row = lax.broadcasted_iota(jnp.int32, ghist_out.shape, 0)
-    ghist_out[...] = jnp.where(hist_row == gsl[...], gpeak_row[...], gh[...])
+    hist_row = lax.broadcasted_iota(jnp.int32, (16, width), 0)
+    pack_out[16:32, :] = jnp.where(hist_row == gsl[...], gpeak_row[...], gh[...])
     h4_arrival().wait_recv()
     hist_row = lax.broadcasted_iota(jnp.int32, hist_out.shape, 0)
     hist_out[...] = jnp.where(hist_row == sl[:, : nc * LANES], peak_row[...], ch[...])
@@ -468,7 +468,7 @@
     for i in range(1, nc):
         frm = (zp + i) % nc
         total = total + rb[frm].astype(jnp.float32)
-    wgrad_out[...] = total[:, :width] / (row_scale * gscale) * factor
+    pack_out[0:16, :] = total[:, :width] / (row_scale * gscale)
 
     for a, done in (
         (g.at[pl.ds(0, 7 * nc)], sg.at[0]),
@@ -486,7 +486,7 @@
     p5_all().wait_send()
 
 
-def fused(acts, grads, ahist, ghist, owner, slots, nz, nx, factor):
+def fused(acts, grads, ahist, ghist, owner, slots, nz, nx):
     rows, model = acts.shape
     width, tokens = grads.shape
     nc, nt = nz // 2, 2 * nx
@@ -538,28 +538,27 @@
     vspec = pl.BlockSpec(memory_space=pltpu.VMEM)
     anyspec = pl.BlockSpec(memory_space=pl.ANY)
     return pl.pallas_call(
-        functools.partial(kernel, nz, nx, factor),
+        functools.partial(kernel, nz, nx),
         out_shape=[
-            jax.ShapeDtypeStruct((16, width), f32),
+            jax.ShapeDtypeStruct((32, width), f32),
             jax.ShapeDtypeStruct((16, model), f32),
-            jax.ShapeDtypeStruct((16, width), f32),
         ],
         in_specs=[anyspec] * 6,
-        out_specs=[vspec] * 3,
+        out_specs=[vspec] * 2,
         scratch_shapes=scratch,
         compiler_params=pltpu.CompilerParams(
-            collective_id=0, has_side_effects=True, vmem_limit_bytes=55100 * 1024
+            collective_id=0, has_side_effects=True, vmem_limit_bytes=60 * 1024 * 1024
         ),
     )(acts, grads, ahist, ghist, owner, slots)
 
 
 def body(nz, nx, activations, gradients, act_history, grad_history, owner_rank, history_slot):
     factor = 1.0 / math.sqrt(gradients.shape[0] * lax.axis_size("dp"))
-    weight_grad, act_history_out, grad_history_out = fused(
+    packed, act_history_out = fused(
         activations, gradients.T, act_history, grad_history,
-        owner_rank.reshape(1, -1), history_slot, nz, nx, factor,
+        owner_rank.reshape(1, -1), history_slot, nz, nx,
     )
-    return (weight_grad, act_history_out[None], grad_history_out)
+    return (packed[:16] * factor, jnp.abs(act_history_out)[None], jnp.abs(packed[16:]))
 
 
 def solution(mesh):

time: 64.4 us -> 63.2 us (0.981)
  local copies, waits for them, and re-layouts: 4.14 us -> 0 us
  other arithmetic: 0 us -> 2.94 us
    unnamed x7 -> x0, local copies, waits for them, and re-layouts: 4.14 us -> none
    broadcast_in_dim x0 -> x1, other arithmetic: none -> 1.47 us  [body(): jnp.abs(act_history_out)[None]]
    abs x0 -> x1, other arithmetic: none -> 1.47 us  [body(): jnp.abs(packed[16:])]
where the time goes in v5:
time: 63.2 us; the launch traced here: 62.9 us
  Pallas kernels  59.4 us (94%)
  other arithmetic  2.94 us (5%)
  between operations  0.64 us (1%)
    pallas_call x1, Pallas kernels, fused(): pl.pallas_call(functools.partial(kernel, nz, nx), out_shape=[jax.ShapeDty...  59.4 us
    broadcast_in_dim x1, other arithmetic, body(): jnp.abs(act_history_out)[None]  1.47 us
    abs x1, other arithmetic, body(): jnp.abs(packed[16:])  1.47 us

profile of v5, /device:TPU:4, one launch (start us, length us, event | category | flops | bytes accessed | tf_op | source)
XLA Modules:
  0.0 62.9 jit_solution(13789259394073288186)
XLA Ops:
  0.6 59.4 %shard_map.85 = (f32[32,684]{1,0:T(8,128)}, f32[16,1024]{1,0:T(8,128)}) custom-call(bf16[256,1024]{1,0:T(8,128)(2,1)} %acts.1, bf16[684,2048]{1,0:T(8,128)(2,1)} %bitcast.4, f32[1,16,1024]{2,1,0:T(8,128)} %ahist.1, f32[16,684]{1,0:T(8,128)} %ghist.1, s32[1,1024]{1,0:T(1,128)} %bitcast.5, s32[6496]{0:T(1024)} %slots.1), custom_call_target="tpu_custom_call" | custom-call | tf_op jit(solution)/shard_map/pallas_call | solution.py:540
  60.0 1.5 %slice_abs_fusion = (f32[16,684]{1,0:T(8,128)}, f32[16,684]{1,0:T(8,128)}) fusion(f32[32,684]{1,0:T(8,128)} %get-tuple-element.5), kind=kLoop, calls=%fused_computation.1 | loop fusion | flops 21888 | bytes 175104 | tf_op jit(solution)/shard_map/abs | solution.py:561
  61.5 1.5 %abs_bitcast_fusion = f32[1,16,1024]{2,1,0:T(8,128)} fusion(f32[16,1024]{1,0:T(8,128)} %get-tuple-element.6), kind=kLoop, calls=%fused_computation | loop fusion | flops 16384 | bytes 131072 | tf_op jit(solution)/shard_map/broadcast_in_dim | solution.py:561

commit v6 on v5

--- a/solution.py
+++ b/solution.py
@@ -421,7 +421,7 @@
         def _():
             tokens_wait()
 
-        @pl.when(jnp.logical_and(s >= 2, s < nc - 1))
+        @pl.when(jnp.logical_and(s >= 2, jnp.logical_or(s < nc - 1, zp > 0)))
         def _():
             finish_quad(s - 2)
 
@@ -436,7 +436,10 @@
     last = nc - 1
     finish_r1(last)
     if nc > 2:
-        finish_quad(last - 2)
+        @pl.when(zp == 0)
+        def _():
+            finish_quad(last - 2)
+
     h3_all().wait_recv()
     h4_copy().start()
     if nc > 1:

time: 63.2 us -> 62.8 us (level)
  the two profiles are of different devices: /device:TPU:4 before, /device:TPU:6 now
where the time goes in v6:
time: 62.8 us; the launch traced here: 62.6 us
  Pallas kernels  59 us (94%)
  other arithmetic  2.94 us (5%)
  between operations  0.64 us (1%)
    pallas_call x1, Pallas kernels, fused(): pl.pallas_call(functools.partial(kernel, nz, nx), out_shape=[jax.ShapeDty...  59 us
    broadcast_in_dim x1, other arithmetic, body(): jnp.abs(act_history_out)[None]  1.47 us
    abs x1, other arithmetic, body(): jnp.abs(packed[16:])  1.47 us

profile of v6, /device:TPU:6, one launch (start us, length us, event | category | flops | bytes accessed | tf_op | source)
XLA Modules:
  0.0 62.6 jit_solution(609557127492324686)
XLA Ops:
  0.6 59.0 %shard_map.85 = (f32[32,684]{1,0:T(8,128)}, f32[16,1024]{1,0:T(8,128)}) custom-call(bf16[256,1024]{1,0:T(8,128)(2,1)} %acts.1, bf16[684,2048]{1,0:T(8,128)(2,1)} %bitcast.4, f32[1,16,1024]{2,1,0:T(8,128)} %ahist.1, f32[16,684]{1,0:T(8,128)} %ghist.1, s32[1,1024]{1,0:T(1,128)} %bitcast.5, s32[6496]{0:T(1024)} %slots.1), custom_call_target="tpu_custom_call" | custom-call | tf_op jit(solution)/shard_map/pallas_call | solution.py:543
  59.7 1.5 %slice_abs_fusion = (f32[16,684]{1,0:T(8,128)}, f32[16,684]{1,0:T(8,128)}) fusion(f32[32,684]{1,0:T(8,128)} %get-tuple-element.5), kind=kLoop, calls=%fused_computation.1 | loop fusion | flops 21888 | bytes 175104 | tf_op jit(solution)/shard_map/abs | solution.py:564
  61.1 1.5 %abs_bitcast_fusion = f32[1,16,1024]{2,1,0:T(8,128)} fusion(f32[16,1024]{1,0:T(8,128)} %get-tuple-element.6), kind=kLoop, calls=%fused_computation | loop fusion | flops 16384 | bytes 131072 | tf_op jit(solution)/shard_map/broadcast_in_dim | solution.py:564
